TPU v7x, 32 devices: a whole 2x2x4 slice. The times are simulated.
32 devices in a mesh: grp: 2 (over y), row: 4 (over z), head: 2 (over x), br: 2 (over core).
Axes of the slice: x: 2, y: 2, z: 4, core: 2. Of those that a mesh axis runs over, the one named last changes fastest.
Arguments:
- pair_acts: float32 [16, 8, 128], P(('grp', 'row', 'head')), parts along dimension 0, may hold values from -6 to 6
- alignment: float32 [64, 8, 256], P(('grp', 'br'), ('row', 'head')), parts along dimension 0, may hold values from -6 to 6
- align_mask: int32 [64, 8], P('grp', ('row', 'head')), parts along dimension 0, may hold values from 0 to 1
- residue_mask: int32 [16], P('grp'), parts along dimension 0, may hold values from 0 to 1, as said below
- align_gain: float32 [256], replicated, may hold values from 0.25 to 1.75
- outer_in: float32 [256, 64], replicated, may hold values from -0.375 to 0.375
- outer_out: float32 [1024, 128], replicated, may hold values from -1 to 1
- tri_gain: float32 [2, 128], replicated, may hold values from 0.25 to 1.75
- tri_in: float32 [2, 128, 4, 128], P(None, None, 'br'), may hold values from -5 to 5
- tri_bias: float32 [2, 128, 4], P(None, None, 'br'), may hold values from -0.5 to 0.5
- tri_out: float32 [2, 4, 32, 128], P(None, 'br'), may hold values from -0.5 to 0.5
- pair_cotangent: float32 [16, 8, 128], P(('grp', 'row', 'head')), parts along dimension 0, may hold values from -6 to 6
Outputs:
- pair_out: float32 [16, 8, 128], P(('grp', 'row', 'head')), parts along dimension 0
- pair_grad: float32 [16, 8, 128], P(('grp', 'row', 'head')), parts along dimension 0
There are 2 independent parts, one for each index of `grp`. A program takes and returns all parts, laid end to end along the dimension named above; an argument that names none is the same for every part. Nothing has to cross between parts.
Inputs may be any that keep to these rules, and one draw needn't show every extreme that they name: `residue_mask`: 1 at residue 0, and 0 at one or more residues; `align_mask`: 1 at every residue of sequence 0 of each part.
All inputs are finite; a program needn't handle non-finite values.
Results may differ from a plain program's by a relative error of at most 0.0003.
Values sent between devices are 32-bit elements; how exact they have to be, the bound alone decides.
No kernel may reach another device: no remote copies, remote signals or barrier semaphores. Data moves between devices by JAX's collectives and lax.ppermute only.
A program may use at most 64 MiB of HBM per device.

v0:
```python
import functools

import jax
import jax.numpy as jnp
from jax import lax
from jax.experimental import pallas as pl
from jax.experimental.pallas import tpu as pltpu
from jax.sharding import PartitionSpec as P


OPC = 32


PRECISE = lax.Precision.HIGHEST
EPSILON = 1e-05
MASK_SHIFT = 1000000000.0


def normalize(values, scales):
    average = jnp.mean(values, axis=-1, keepdims=True)
    centred = values - average
    spread = jnp.mean(centred * centred, axis=-1, keepdims=True)
    return centred * lax.rsqrt(spread + EPSILON) * scales


def core_total(values):
    return lax.psum(values, "br")


def reorient(values):
    turned = jnp.swapaxes(values, 0, 1)
    return lax.all_to_all(turned, ("row", "head"), split_axis=0, concat_axis=1, tiled=True)


def prepare(values, scales, weight_in, weight_bias):
    normed = normalize(values, scales)
    projected = jnp.einsum("ijc,chd->ijhd", normed, weight_in, precision=PRECISE)
    bias_local = jnp.einsum("jkc,ch->hjk", normed, weight_bias, precision=PRECISE)
    return (projected, bias_local)


def attend(projected, bias_full, key_shift, weight_out):
    head_size = projected.shape[-1] // 4
    queries = projected[..., :head_size]
    key_proj = projected[..., head_size : 2 * head_size]
    value_proj = projected[..., 2 * head_size : 3 * head_size]
    gating = projected[..., 3 * head_size :]
    logits = jnp.einsum("ijhd,ikhd->ihjk", queries, key_proj, precision=PRECISE) * head_size ** (
        -0.5
    )
    logits = logits + bias_full[None] + key_shift
    attention = jax.nn.softmax(logits, axis=-1)
    attended = jnp.einsum("ihjk,ikhd->ijhd", attention, value_proj, precision=PRECISE)
    gated_out = jax.nn.sigmoid(gating) * attended
    return jnp.einsum("ijhd,hdc->ijc", gated_out, weight_out, precision=PRECISE)


def tri_forward(rows_in, scales, weight_in, weight_bias, weight_out, key_shift, pair_mask):

    def local_prep(values):
        return prepare(values, scales, weight_in, weight_bias)

    (projected, bias_local), pull_prep = jax.vjp(local_prep, rows_in)
    bias_full = lax.all_gather(bias_local, ("row", "head"), axis=1, tiled=True)

    def local_attend(proj_in, bias_in):
        return attend(proj_in, bias_in, key_shift, weight_out)

    partial_out, pull_attend = jax.vjp(local_attend, projected, bias_full)
    total_out = core_total(partial_out)
    return (rows_in + total_out * pair_mask, (pull_prep, pull_attend))


def tri_backward(grad_out, saved, pair_mask):
    pull_prep, pull_attend = saved
    grad_proj, grad_bias = pull_attend(grad_out * pair_mask)
    grad_local = lax.psum_scatter(grad_bias, ("row", "head"), scatter_dimension=1, tiled=True)
    (grad_rows,) = pull_prep((grad_proj, grad_local))
    return grad_out + core_total(grad_rows)


def body(
    pair_acts,
    alignment,
    align_mask,
    residue_mask,
    align_gain,
    outer_in,
    outer_out,
    tri_gain,
    tri_in,
    tri_bias,
    tri_out,
    pair_cotangent,
):
    row_count = pair_acts.shape[0]
    live = residue_mask.astype(jnp.float32)
    key_shift = (live - 1.0) * MASK_SHIFT
    row_live = lax.dynamic_slice_in_dim(
        live, lax.axis_index(("row", "head")) * row_count, row_count, 0
    )
    pair_mask = row_live[:, None, None] * live[None, :, None]
    seq_count = alignment.shape[0]
    mask_all = align_mask.astype(jnp.float32)
    mask_own = lax.dynamic_slice_in_dim(mask_all, lax.axis_index("br") * seq_count, seq_count, 0)
    normed = normalize(alignment, align_gain)
    projected = jnp.einsum("snc,ck->snk", normed, outer_in, precision=PRECISE)
    left_part = projected[..., :OPC] * mask_own[..., None]
    right_part = jnp.swapaxes(projected[..., OPC:] * mask_own[..., None], 1, 2)
    right_all, mask_cols = (
        lax.all_gather(right_part, ("row", "head"), axis=2, tiled=True),
        lax.all_gather(mask_all, ("row", "head"), axis=1, tiled=True),
    )
    counts = jnp.einsum("si,sj->ij", mask_all, mask_cols, precision=PRECISE)
    table = outer_out.reshape(OPC, OPC, outer_out.shape[-1])
    mixed_left = jnp.einsum("sip,pqc->siqc", left_part, table, precision=PRECISE)
    partial_outer = jnp.einsum("siqc,sqj->ijc", mixed_left, right_all, precision=PRECISE)
    outer_sum = core_total(partial_outer)
    pair_one = pair_acts + outer_sum / counts[..., None]
    pair_two, saved_start = tri_forward(
        pair_one, tri_gain[0], tri_in[0], tri_bias[0], tri_out[0], key_shift, pair_mask
    )
    turned_two = reorient(pair_two)
    turned_three, saved_end = tri_forward(
        turned_two, tri_gain[1], tri_in[1], tri_bias[1], tri_out[1], key_shift, pair_mask
    )
    pair_out = reorient(turned_three)
    grad_turned = reorient(pair_cotangent)
    grad_turned = tri_backward(grad_turned, saved_end, pair_mask)
    grad_two = reorient(grad_turned)
    pair_grad = tri_backward(grad_two, saved_start, pair_mask)
    return (pair_out, pair_grad)


F32 = jnp.float32
BF16 = jnp.bfloat16
LANES = 128
SUBLANES = 8
NN = (((1,), (0,)), ((), ()))
NT = (((1,), (1,)), ((), ()))
TN = (((0,), (0,)), ((), ()))


def split2(values):
    high = values.astype(BF16)
    return high, (values - high.astype(F32)).astype(BF16)


def dot(left, right, dims=NN):
    return lax.dot_general(left, right, dims, preferred_element_type=F32)


def times_stacked(values, stacked):
    high, low = split2(values)
    depth = stacked.shape[0] // 2
    return dot(jnp.concatenate([high, high], axis=1), stacked) + dot(low, stacked[:depth])


def fold(product, rows, columns):
    return product[:rows, :columns] + product[:rows, columns:] + product[rows:, :columns]


def times_stacked_t(values, stacked):
    high, low = split2(values)
    product = dot(jnp.concatenate([high, low], axis=0), stacked, NT)
    return fold(product, values.shape[0], stacked.shape[0] // 2)


def times_beside(values, beside):
    high, low = split2(values)
    product = dot(jnp.concatenate([high, low], axis=0), beside)
    return fold(product, values.shape[0], beside.shape[1] // 2)


def centre(values):
    average = jnp.mean(values, axis=-1, keepdims=True)
    centred = values - average
    scale = lax.rsqrt(jnp.mean(centred * centred, axis=-1, keepdims=True) + EPSILON)
    return centred * scale, scale


def regroup(blocks, width):
    groups = blocks[0].shape[1] // width
    return [
        jnp.concatenate([block[:, g * width : (g + 1) * width] for block in blocks], axis=1)
        for g in range(groups)
    ]


def project_kernel(*refs):
    count = (len(refs) - 2) // 2
    sources, out_ref, held, sems = refs[:count], refs[count], refs[count + 1 : -1], refs[-1]
    copies = [
        pltpu.make_async_copy(source, place, sems.at[k])
        for k, (source, place) in enumerate(zip(sources, held))
    ]
    for copy in copies:
        copy.start()
    for copy in copies:
        copy.wait()
    project_part(*held, out_ref)


def project_part(align_ref, mask_ref, gain_ref, proj_ref, pair_ref, cot_ref, out_ref):
    part = lax.axis_index("br")
    seqs, _, width = align_ref.shape
    rows = seqs // 2
    line = mask_ref[...].astype(F32)
    sequence = lax.broadcasted_iota(jnp.int32, (seqs, line.shape[1]), 0) + part * seqs
    lane = lax.broadcasted_iota(jnp.int32, (seqs, line.shape[1]), 1)
    own = jnp.sum(jnp.where(sequence == lane, line, 0.0), axis=1, keepdims=True)
    values = jnp.reshape(align_ref[...], (seqs, width))
    normed, _ = centre(values)
    stacked = jnp.concatenate(split2(proj_ref[...]), axis=0)
    projected = times_stacked_t(normed * gain_ref[...], stacked) * own
    out_ref[0:rows, :] = jnp.concatenate([projected[:rows], projected[rows:]], axis=1)
    count = pair_ref.shape[1]
    out_ref[rows : rows + count, :] = jnp.where(part == 0, pair_ref[0], cot_ref[0])
    rest = jnp.zeros((1, LANES - line.shape[1]), F32)
    line = jnp.concatenate([line, rest], axis=1)
    out_ref[rows + count :, :] = jnp.broadcast_to(line, (SUBLANES, LANES))


def weights_kernel(layer, gain_ref, own_in, peer_in, own_bias, peer_bias, own_out, peer_out, in_ref, out_ref):
    first = lax.axis_index("br") == 0
    heads, width = own_in.shape[2:]
    size = width // 4
    blocks, lines, ends = [], [], []
    for half in range(2):
        pick = first if half == 0 else jnp.logical_not(first)
        for h in range(heads):
            blocks.append(jnp.where(pick, own_in[layer, :, h, :], peer_in[layer, :, h, :]))
            bias = jnp.where(pick, own_bias[layer, h : h + 1, :], peer_bias[layer, h : h + 1, :])
            lines.append(jnp.broadcast_to(bias, (size, bias.shape[1])))
            ends.append(jnp.where(pick, own_out[layer, h], peer_out[layer, h]))
    table = jnp.concatenate(regroup(blocks, size) + [jnp.concatenate(lines, axis=0).T], axis=1)
    gain = gain_ref[layer : layer + 1, :]
    table = table * jnp.broadcast_to(gain, (gain.shape[1], gain.shape[1])).T[:, :1]
    in_ref[...] = jnp.concatenate(split2(table), axis=0)
    out_ref[...] = jnp.concatenate(split2(jnp.concatenate(ends, axis=0)), axis=0)


def table_kernel(table_ref, live_ref, out_ref, rows_ref):
    for q in range(OPC):
        rows = table_ref[pl.ds(q, OPC, stride=OPC), :]
        out_ref[q * OPC : (q + 1) * OPC, :] = jnp.concatenate(split2(rows), axis=1)
    sub = lax.broadcasted_iota(jnp.int32, rows_ref.shape, 0)
    live = jnp.zeros(rows_ref.shape, F32)
    for k in range(rows_ref.shape[0]):
        live = jnp.where(sub == k, live_ref[k].astype(F32), live)
    rows_ref[...] = live


def part_kernel(
    heads, own_ref, peer_ref, live_ref, in_0, end_0, in_1, end_1, table_ref, out_ref, grad_ref,
    mixed, keys, vals, lines, turn, many, more,
):
    me = lax.axis_index(("row", "head"))
    first = lax.axis_index("br") == 0
    n = own_ref.shape[0]
    count = n
    rows = own_ref.shape[1] - count - SUBLANES
    total = n * n
    width = live_ref.shape[1]
    in_ref, end_ref = (in_0, in_1), (end_0, end_1)
    heads_wide = end_0.shape[0] // 2
    size = heads_wide // heads

    def taken(start, stop, r, flip):
        slot = jnp.bitwise_xor(me, r)
        mine, other = own_ref[slot, start:stop, :], peer_ref[slot, start:stop, :]
        return jnp.where(first, other, mine) if flip else jnp.where(first, mine, other)

    def transpose_rows(values):
        turn[...] = values
        return jnp.concatenate([turn[pl.ds(j, n, stride=n), :] for j in range(n)], axis=0)

    live = live_ref[...]
    pair_mask = jnp.concatenate([live * live_ref[i : i + 1, :] for i in range(n)], axis=0)
    shift = [(live_ref[k : k + 1, :] - 1.0) * MASK_SHIFT for k in range(n)]

    lefts, rights = [], []
    for flip in (False, True):
        blocks = [taken(0, rows, r, flip) for r in range(n)]
        pieces = regroup(blocks, OPC)
        lefts += [pieces[0], pieces[2]]
        rights += [pieces[1], pieces[3]]
    left, right = jnp.concatenate(lefts, axis=0), jnp.concatenate(rights, axis=0)
    left_high, left_low = split2(left)
    right_high, right_low = split2(right)
    product = dot(
        jnp.concatenate([right_high, right_high, right_low], axis=0),
        jnp.concatenate([left_high, left_low, left_high], axis=0),
        TN,
    )
    per = LANES // OPC
    chunks = []
    for part in range(n // per):
        mixed[part] = product[:, part * LANES : (part + 1) * LANES]
        lots = []
        for base in range(0, OPC, per):
            lots.append(regroup([mixed[part, pl.ds(base + g, n, stride=OPC), :] for g in range(per)], OPC))
        chunks += [[lot[g] for lot in lots] for g in range(per)]
    spread = jnp.concatenate([jnp.concatenate(c, axis=1) for c in chunks], axis=0)
    outer = times_beside(spread, table_ref[...])
    seen = jnp.concatenate(
        [own_ref[jnp.bitwise_xor(me, r), rows + count : rows + count + 1, :] for r in range(n)], axis=0
    )
    both = jnp.concatenate([seen * seen[i : i + 1] for i in range(n)], axis=0)
    counts = dot(both.astype(BF16), jnp.ones((LANES, width), BF16))
    pair = jnp.concatenate([taken(rows, rows + count, r, False) for r in range(n)], axis=0)
    cot = jnp.concatenate([taken(rows, rows + count, r, True) for r in range(n)], axis=0)
    pair_one = pair + outer / counts

    same = lax.broadcasted_iota(jnp.int32, (heads_wide, heads_wide), 0) // size
    head = lax.broadcasted_iota(jnp.int32, (heads_wide, heads_wide), 1) // size
    ones = jnp.where(same == head, 1.0, 0.0).astype(BF16)
    ones = jnp.concatenate([ones, ones], axis=0)
    factor = size ** (-0.5)

    def head_sums(values):
        return dot(jnp.concatenate(split2(values), axis=1), ones)

    def block(values, i):
        return values[i * n : (i + 1) * n]

    def forward(layer, entry):
        hat, scale = centre(entry)
        projected = times_stacked(hat, in_ref[layer][...])
        q, k, v, gate, bias = [
            projected[:, t * heads_wide : (t + 1) * heads_wide] for t in range(5)
        ]
        q = q * factor
        keys[layer], vals[layer] = k, v
        lines[...] = bias
        biases = [lines[pl.ds(kk, n, stride=n), :] + shift[kk] for kk in range(n)]
        logits = head_sums(
            jnp.concatenate(
                [block(q, i) * keys[layer, i * n + kk : i * n + kk + 1, :] for i in range(n) for kk in range(n)],
                axis=0,
            )
        )
        probs, attended = [], []
        for i in range(n):
            own = [block(logits, i * n + kk) + biases[kk] for kk in range(n)]
            top = own[0]
            for item in own[1:]:
                top = jnp.maximum(top, item)
            own = [jnp.exp(item - top) for item in own]
            whole = own[0]
            for item in own[1:]:
                whole = whole + item
            inverse = 1.0 / whole
            own = [item * inverse for item in own]
            probs.append(own)
            mix = own[0] * vals[layer, i * n : i * n + 1, :]
            for kk in range(1, n):
                mix = mix + own[kk] * vals[layer, i * n + kk : i * n + kk + 1, :]
            attended.append(mix)
        attended = jnp.concatenate(attended, axis=0)
        opened = jax.nn.sigmoid(gate)
        update = times_stacked(opened * attended, end_ref[layer][...])
        return entry + update * pair_mask, (hat, scale, q, opened, attended, probs)

    def row_sums(scratch):
        whole = scratch[pl.ds(0, total, stride=n), :]
        for j in range(1, n):
            whole = whole + scratch[pl.ds(j, total, stride=n), :]
        return whole

    def backward(layer, grad, saved):
        hat, scale, q, opened, attended, probs = saved
        pulled = times_stacked_t(grad * pair_mask, end_ref[layer][...])
        d_att = pulled * opened
        d_gate = d_att * attended * (1.0 - opened)
        d_probs = head_sums(
            jnp.concatenate(
                [block(d_att, i) * vals[layer, i * n + kk : i * n + kk + 1, :] for i in range(n) for kk in range(n)],
                axis=0,
            )
        )
        d_q, d_bias = [], [None] * n
        for i in range(n):
            own = [block(d_probs, i * n + kk) for kk in range(n)]
            both_ = [probs[i][kk] * own[kk] for kk in range(n)]
            mean = both_[0]
            for item in both_[1:]:
                mean = mean + item
            piece = None
            for kk in range(n):
                d_logit = both_[kk] - probs[i][kk] * mean
                at = (i * n + kk) * n
                many[at : at + n, :] = d_logit * block(q, i)
                more[at : at + n, :] = probs[i][kk] * block(d_att, i)
                term = d_logit * keys[layer, i * n + kk : i * n + kk + 1, :]
                piece = term if piece is None else piece + term
                d_bias[kk] = d_logit if d_bias[kk] is None else d_bias[kk] + d_logit
            d_q.append(piece)
        d_q = jnp.concatenate(d_q, axis=0) * factor
        d_bias = transpose_rows(jnp.concatenate(d_bias, axis=0) * (1.0 / size))
        d_all = jnp.concatenate([d_q, row_sums(many), row_sums(more), d_gate, d_bias], axis=1)
        d_hat = times_stacked_t(d_all, in_ref[layer][...])
        inner = d_hat - jnp.mean(d_hat, axis=-1, keepdims=True)
        inner = inner - hat * jnp.mean(d_hat * hat, axis=-1, keepdims=True)
        return grad + inner * scale

    pair_two, saved_start = forward(0, pair_one)
    turned, saved_end = forward(1, transpose_rows(pair_two))
    turn[...] = turned
    out_ref[0] = turn[pl.ds(me, n, stride=n), :]
    grad = backward(1, transpose_rows(cot), saved_end)
    grad = backward(0, transpose_rows(grad), saved_start)
    turn[...] = grad
    grad_ref[0] = turn[pl.ds(pl.multiple_of(me * n, SUBLANES), n), :]


def spec(space=pltpu.VMEM):
    return pl.BlockSpec(memory_space=space)


def cost(flops):
    return pl.CostEstimate(flops=flops, bytes_accessed=1 << 20, transcendentals=0)


def limit(mebibytes):
    return pltpu.CompilerParams(vmem_limit_bytes=mebibytes << 20)


def opposite(count, bit):
    return [(k, k ^ bit) for k in range(count)]


def small_body(*args):
    return gathered(*args)


def gathered(
    pair_acts,
    alignment,
    align_mask,
    residue_mask,
    align_gain,
    outer_in,
    outer_out,
    tri_gain,
    tri_in,
    tri_bias,
    tri_out,
    pair_cotangent,
):
    _, n, width = pair_acts.shape
    seqs = alignment.shape[0]
    layers, _, heads, quad = tri_in.shape
    inner = 2 * heads * (quad // 4)
    swap = opposite(2, 1)
    square = n * n
    bias = jnp.swapaxes(tri_bias, 1, 2)
    firsts = (alignment, align_mask.T, align_gain[None], outer_in.T, pair_acts, pair_cotangent)
    payload = pl.pallas_call(
        project_kernel,
        out_shape=jax.ShapeDtypeStruct((seqs // 2 + n + SUBLANES, LANES), F32),
        in_specs=[spec(pltpu.HBM)] * len(firsts),
        out_specs=spec(),
        scratch_shapes=[pltpu.VMEM(v.shape, v.dtype) for v in firsts]
        + [pltpu.SemaphoreType.DMA((len(firsts),))],
        compiler_params=limit(2),
        name="project",
    )(*[pltpu.with_memory_space_constraint(v, pltpu.HBM) for v in firsts])
    table, live_rows = pl.pallas_call(
        table_kernel,
        out_shape=(
            jax.ShapeDtypeStruct((outer_out.shape[0], 2 * width), BF16),
            jax.ShapeDtypeStruct((n, width), F32),
        ),
        in_specs=[spec(), spec(pltpu.SMEM)],
        out_specs=(spec(), spec()),
        compiler_params=limit(4),
        cost_estimate=cost(1 << 22),
        name="table",
    )(outer_out, residue_mask)
    peers = []
    for value in (tri_in, bias, tri_out):
        peers.append(lax.ppermute(value, "br", swap))
    weights = []
    for layer in range(layers):
        weights += pl.pallas_call(
            functools.partial(weights_kernel, layer),
            out_shape=(
                jax.ShapeDtypeStruct((2 * width, 5 * inner), BF16),
                jax.ShapeDtypeStruct((2 * inner, width), BF16),
            ),
            in_specs=[spec()] * 7,
            out_specs=(spec(), spec()),
            compiler_params=limit(4),
            cost_estimate=cost(1 << 22),
        )(tri_gain, tri_in, peers[0], bias, peers[1], tri_out, peers[2])
    held = payload[None]
    steps = []
    for axis in ("head", "row"):
        bit = 1
        while bit < lax.axis_size(axis):
            steps.append((axis, opposite(lax.axis_size(axis), bit)))
            bit *= 2
    for axis, pairs in steps:
        got = lax.ppermute(held, axis, pairs)
        held = jnp.concatenate([held, got], axis=0)
    other = lax.ppermute(held, "br", swap)
    shape = jax.ShapeDtypeStruct((1, n, width), F32)
    return pl.pallas_call(
        functools.partial(part_kernel, 2 * heads),
        out_shape=(shape, shape),
        in_specs=[spec()] * 8,
        out_specs=(spec(), spec()),
        scratch_shapes=[
            pltpu.VMEM((n * OPC // LANES, n * OPC, LANES), F32),
            pltpu.VMEM((layers, square, inner), F32),
            pltpu.VMEM((layers, square, inner), F32),
            pltpu.VMEM((square, inner), F32),
            pltpu.VMEM((square, width), F32),
            pltpu.VMEM((square * n, inner), F32),
            pltpu.VMEM((square * n, inner), F32),
        ],
        compiler_params=limit(8),
        name="part",
    )(held, other, live_rows, *weights, table)


def is_small(mesh, residues, seqs, width, inner):
    group = mesh.shape["row"] * mesh.shape["head"]
    powers = all(mesh.shape[a] & (mesh.shape[a] - 1) == 0 for a in ("row", "head"))
    return (
        powers
        and mesh.shape["br"] == 2
        and residues == group == SUBLANES
        and seqs % (2 * 2 * SUBLANES) == 0
        and seqs <= LANES
        and 4 * OPC == width == inner == LANES
    )


def solution(mesh):
    in_specs = (
        P(("grp", "row", "head"), None, None),
        P(("grp", "br"), ("row", "head"), None),
        P("grp", ("row", "head")),
        P("grp"),
        P(),
        P(),
        P(),
        P(),
        P(None, None, "br", None),
        P(None, None, "br"),
        P(None, "br", None, None),
        P(("grp", "row", "head"), None, None),
    )
    out_specs = (P(("grp", "row", "head"), None, None), P(("grp", "row", "head"), None, None))

    def mapped(*args):
        residues, seqs = args[0].shape[1], args[1].shape[0] // mesh.shape["grp"]
        width, inner = args[0].shape[2], args[10].shape[1] * args[10].shape[2]
        small = is_small(mesh, residues, seqs, width, inner)
        chosen = small_body if small else body
        step = jax.shard_map(chosen, mesh=mesh, in_specs=in_specs, out_specs=out_specs, check_vma=False)
        return step(*args)

    return mapped
```

profile of v0, /device:TPU:0, one launch (start us, length us, event | category | flops | bytes accessed | tf_op | source)
XLA Modules:
  0.0 23.9 jit_solution(12417522944165508709)
XLA Ops:
  0.6 1.4 %project.1 = f32[24,128]{1,0:T(8,128)S(1)} custom-call(f32[16,1,256]{2,1,0:T(1,128)} %refs_0_.1, s32[1,32]{1,0:T(1,128)} %bitcast.14, f32[1,256]{1,0:T(1,128)} %bitcast.13, f32[64,256]{1,0:T(8,128)} %bitcast.12, f32[1,8,128]{2,1,0:T(8,128)} %refs_4_.1, f32[1,8,128]{2,1,0:T(8,128)} %refs_5_.1), custom_call_target="tpu_custom_call" | custom-call | tf_op jit(solution)/shard_map/project/pallas_call | solution.py:459
  2.0 3.0 %collective-permute-start = (f32[1,24,128]{2,1,0:T(8,128)S(1)}, f32[1,24,128]{2,1,0:T(8,128)S(1)}, u32[]{:S(2)}, u32[]{:S(2)}) collective-permute-start(f32[1,24,128]{2,1,0:T(8,128)S(1)} %bitcast.5), channel_id=1, source_target_pairs={{0,2},{2,0},{1,3},{3,1},{4,6},{6,4},{5,7},{7,5},{8,10},{10,8},{9,1... | collective-permute-start | bytes 36872 | tf_op jit(solution)/shard_map/ppermute | solution.py:505
  5.0 1.7 %collective-permute-done = f32[1,24,128]{2,1,0:T(8,128)S(1)} collective-permute-done((f32[1,24,128]{2,1,0:T(8,128)S(1)}, f32[1,24,128]{2,1,0:T(8,128)S(1)}, u32[]{:S(2)}, u32[]{:S(2)}) %collective-permute-start) | collective-permute-done | bytes 12320 | tf_op jit(solution)/shard_map/ppermute | solution.py:505
  6.7 2.1 %collective-permute-start.1 = (f32[2,24,128]{2,1,0:T(8,128)S(1)}, f32[2,24,128]{2,1,0:T(8,128)S(1)}, u32[]{:S(2)}, u32[]{:S(2)}) collective-permute-start(f32[2,24,128]{2,1,0:T(8,128)S(1)} %pad_maximum_fusion.2), channel_id=1, source_target_pairs={{0,4},{4,0},{8,12},{12,8},{1,5},{5,1},{9,13},{13,9},{2,6},{6,2},{1... | collective-permute-start | bytes 73736 | tf_op jit(solution)/shard_map/ppermute | solution.py:505
  8.8 0.0 collective-permute-start.4
  8.8 1.8 %collective-permute-done.1 = f32[2,24,128]{2,1,0:T(8,128)S(1)} collective-permute-done((f32[2,24,128]{2,1,0:T(8,128)S(1)}, f32[2,24,128]{2,1,0:T(8,128)S(1)}, u32[]{:S(2)}, u32[]{:S(2)}) %collective-permute-start.1) | collective-permute-done | bytes 24608 | tf_op jit(solution)/shard_map/ppermute | solution.py:505
  10.6 0.0 copy-start.2
  10.6 0.0 copy-start.3
  10.6 3.1 %collective-permute-start.2 = (f32[4,24,128]{2,1,0:T(8,128)S(1)}, f32[4,24,128]{2,1,0:T(8,128)S(1)}, u32[]{:S(2)}, u32[]{:S(2)}) collective-permute-start(f32[4,24,128]{2,1,0:T(8,128)S(1)} %pad_maximum_fusion.1), channel_id=1, source_target_pairs={{0,8},{4,12},{8,0},{12,4},{1,9},{5,13},{9,1},{13,5},{2,10},{6,14},... | collective-permute-start | bytes 147464 | tf_op jit(solution)/shard_map/ppermute | solution.py:505
  13.7 2.1 %collective-permute-done.2 = f32[4,24,128]{2,1,0:T(8,128)S(1)} collective-permute-done((f32[4,24,128]{2,1,0:T(8,128)S(1)}, f32[4,24,128]{2,1,0:T(8,128)S(1)}, u32[]{:S(2)}, u32[]{:S(2)}) %collective-permute-start.2) | collective-permute-done | bytes 49184 | tf_op jit(solution)/shard_map/ppermute | solution.py:505
  15.8 0.0 copy-start.5
  15.8 0.1 collective-permute-start.3
  15.9 0.0 copy-done.2
  15.9 0.5 %collective-permute-start.6 = (f32[2,2,32,128]{3,2,1,0:T(8,128)S(1)}, f32[2,2,32,128]{3,2,1,0:T(8,128)S(1)}, u32[]{:S(2)}, u32[]{:S(2)}) collective-permute-start(f32[2,2,32,128]{3,2,1,0:T(8,128)S(1)} %copy-done.2), channel_id=1, source_target_pairs={{0,1},{1,0},{2,3},{3,2},{4,5},{5,4},{6,7},{7,6},{8,9},{9,8},{10,11... | collective-permute-start | bytes 196616 | tf_op jit(solution)/shard_map/ppermute | solution.py:483
  16.4 0.0 copy-done.3
  16.4 0.0 copy-start
  16.4 0.1 collective-permute-start.5
  16.5 0.0 copy-done.5
  16.5 0.0 copy-start.1
  16.5 1.0 %copy-done.1 = f32[1024,128]{1,0:T(8,128)S(1)} copy-done((f32[1024,128]{1,0:T(8,128)S(1)}, f32[1024,128]{1,0:T(8,128)}, u32[]{:S(2)}) %copy-start.1) | copy-done | bytes 524312
  17.6 0.0 copy-start.4
  17.6 0.8 %table.1 = (bf16[1024,256]{1,0:T(8,128)(2,1)S(1)}, f32[8,128]{1,0:T(8,128)S(1)}) custom-call(f32[1024,128]{1,0:T(8,128)S(1)} %copy-done.1, s32[8]{0:T(128)S(1)} %copy-done.5), custom_call_target="tpu_custom_call" | custom-call | flops 4194304 | bytes 1048576 | tf_op jit(solution)/shard_map/table/pallas_call | solution.py:469
  18.4 0.0 collective-permute-done.5.peer_bias
  18.4 0.0 collective-permute-done.6.peer_out
  18.4 0.0 collective-permute-done.4.peer_in
  18.4 0.0 copy-done
  18.4 0.0 copy-done.4
  18.5 0.5 %shard_map.132 = (bf16[256,640]{1,0:T(8,128)(2,1)S(1)}, bf16[256,128]{1,0:T(8,128)(2,1)S(1)}) custom-call(f32[2,128]{1,0:T(2,128)S(1)} %copy-done.4, f32[2,128,2,128]{3,2,1,0:T(2,128)S(1)} %copy-done, f32[2,128,2,128]{3,2,1,0:T(2,128)S(1)} %collective-permute-done.4.peer_in, f32[2,2,128]{2,1,0:T(2,128)S(1)} %bitcast.10, ...), custom_call_target="tpu_custom_call" | custom-call | flops 4194304 | bytes 1048576 | tf_op jit(solution)/shard_map/pallas_call | solution.py:486
  19.0 0.5 %shard_map.131 = (bf16[256,640]{1,0:T(8,128)(2,1)S(1)}, bf16[256,128]{1,0:T(8,128)(2,1)S(1)}) custom-call(f32[2,128]{1,0:T(2,128)S(1)} %copy-done.4, f32[2,128,2,128]{3,2,1,0:T(2,128)S(1)} %copy-done, f32[2,128,2,128]{3,2,1,0:T(2,128)S(1)} %collective-permute-done.4.peer_in, f32[2,2,128]{2,1,0:T(2,128)S(1)} %bitcast.11, ...), custom_call_target="tpu_custom_call" | custom-call | flops 4194304 | bytes 1048576 | tf_op jit(solution)/shard_map/pallas_call | solution.py:486
  19.5 0.0 collective-permute-done.3.peer_ref
  19.6 4.4 %part.1 = (f32[1,8,128]{2,1,0:T(8,128)}, f32[1,8,128]{2,1,0:T(8,128)}) custom-call(f32[8,24,128]{2,1,0:T(8,128)S(1)} %pad_maximum_fusion.own_ref, f32[8,24,128]{2,1,0:T(8,128)S(1)} %collective-permute-done.3.peer_ref, f32[8,128]{1,0:T(8,128)S(1)} %get-tuple-element.8.live_ref, bf16[256,640]{1,0:T(8,128)(2,1)S(1)} %get-tuple-element.9.in_0, ...), custom_call_target="tpu_custom_call" | custom-call | tf_op jit(solution)/shard_map/part/pallas_call | solution.py:509
  (3 shorter events, 0.0 us)
Async XLA Ops:
  2.0 4.7 %collective-permute-start = (f32[1,24,128]{2,1,0:T(8,128)S(1)}, f32[1,24,128]{2,1,0:T(8,128)S(1)}, u32[]{:S(2)}, u32[]{:S(2)}) collective-permute-start(f32[1,24,128]{2,1,0:T(8,128)S(1)} %bitcast.5), channel_id=1, source_target_pairs={{0,2},{2,0},{1,3},{3,1},{4,6},{6,4},{5,7},{7,5},{8,10},{10,8},{9,1... | collective-permute-start | bytes 36872 | tf_op jit(solution)/shard_map/ppermute | solution.py:505
  6.7 3.9 %collective-permute-start.1 = (f32[2,24,128]{2,1,0:T(8,128)S(1)}, f32[2,24,128]{2,1,0:T(8,128)S(1)}, u32[]{:S(2)}, u32[]{:S(2)}) collective-permute-start(f32[2,24,128]{2,1,0:T(8,128)S(1)} %pad_maximum_fusion.2), channel_id=1, source_target_pairs={{0,4},{4,0},{8,12},{12,8},{1,5},{5,1},{9,13},{13,9},{2,6},{6,2},{1... | collective-permute-start | bytes 73736 | tf_op jit(solution)/shard_map/ppermute | solution.py:505
  8.8 9.6 %collective-permute-start.4 = (f32[2,128,2,128]{3,2,1,0:T(2,128)}, f32[2,128,2,128]{3,2,1,0:T(2,128)S(1)}, u32[]{:S(2)}, u32[]{:S(2)}) collective-permute-start(f32[2,128,2,128]{3,2,1,0:T(2,128)} %own_in.3), channel_id=1, source_target_pairs={{0,1},{1,0},{2,3},{3,2},{4,5},{5,4},{6,7},{7,6},{8,9},{9,8},{10,11... | collective-permute-start | bytes 786440 | tf_op jit(solution)/shard_map/ppermute | solution.py:483
  10.6 5.3 %copy-start.2 = (f32[2,2,32,128]{3,2,1,0:T(8,128)S(1)}, f32[2,2,32,128]{3,2,1,0:T(8,128)}, u32[]{:S(2)}) copy-start(f32[2,2,32,128]{3,2,1,0:T(8,128)} %own_out.3) | copy-start | bytes 196612
  10.6 5.8 %copy-start.3 = (f32[2,128,2]{1,2,0:T(2,128)S(1)}, f32[2,128,2]{1,2,0:T(2,128)}, u32[]{:S(2)}) copy-start(f32[2,128,2]{1,2,0:T(2,128)} %param.21) | copy-start | bytes 6148
  10.6 5.2 %collective-permute-start.2 = (f32[4,24,128]{2,1,0:T(8,128)S(1)}, f32[4,24,128]{2,1,0:T(8,128)S(1)}, u32[]{:S(2)}, u32[]{:S(2)}) collective-permute-start(f32[4,24,128]{2,1,0:T(8,128)S(1)} %pad_maximum_fusion.1), channel_id=1, source_target_pairs={{0,8},{4,12},{8,0},{12,4},{1,9},{5,13},{9,1},{13,5},{2,10},{6,14},... | collective-permute-start | bytes 147464 | tf_op jit(solution)/shard_map/ppermute | solution.py:505
  15.8 0.7 %copy-start.5 = (s32[8]{0:T(128)S(1)}, s32[8]{0:T(128)}, u32[]{:S(2)}) copy-start(s32[8]{0:T(128)} %live_ref.1) | copy-start | bytes 100
  15.8 3.7 %collective-permute-start.3 = (f32[8,24,128]{2,1,0:T(8,128)S(1)}, f32[8,24,128]{2,1,0:T(8,128)S(1)}, u32[]{:S(2)}, u32[]{:S(2)}) collective-permute-start(f32[8,24,128]{2,1,0:T(8,128)S(1)} %pad_maximum_fusion.own_ref), channel_id=1, source_target_pairs={{0,1},{1,0},{2,3},{3,2},{4,5},{5,4},{6,7},{7,6},{8,9},{9,8},{10,11... | collective-permute-start | bytes 294920 | tf_op jit(solution)/shard_map/ppermute | solution.py:507
  15.9 2.5 %collective-permute-start.6 = (f32[2,2,32,128]{3,2,1,0:T(8,128)S(1)}, f32[2,2,32,128]{3,2,1,0:T(8,128)S(1)}, u32[]{:S(2)}, u32[]{:S(2)}) collective-permute-start(f32[2,2,32,128]{3,2,1,0:T(8,128)S(1)} %copy-done.2), channel_id=1, source_target_pairs={{0,1},{1,0},{2,3},{3,2},{4,5},{5,4},{6,7},{7,6},{8,9},{9,8},{10,11... | collective-permute-start | bytes 196616 | tf_op jit(solution)/shard_map/ppermute | solution.py:483
  16.4 2.0 %copy-start = (f32[2,128,2,128]{3,2,1,0:T(2,128)S(1)}, f32[2,128,2,128]{3,2,1,0:T(2,128)}, u32[]{:S(2)}) copy-start(f32[2,128,2,128]{3,2,1,0:T(2,128)} %own_in.3) | copy-start | bytes 786436
  16.4 2.0 %collective-permute-start.5 = (f32[2,2,128]{2,1,0:T(2,128)S(1)}, f32[2,2,128]{2,1,0:T(2,128)S(1)}, u32[]{:S(2)}, u32[]{:S(2)}) collective-permute-start(f32[2,2,128]{2,1,0:T(2,128)S(1)} %bitcast.9), channel_id=1, source_target_pairs={{0,1},{1,0},{2,3},{3,2},{4,5},{5,4},{6,7},{7,6},{8,9},{9,8},{10,11... | collective-permute-start | bytes 6152 | tf_op jit(solution)/shard_map/ppermute | solution.py:483
  16.5 1.0 %copy-start.1 = (f32[1024,128]{1,0:T(8,128)S(1)}, f32[1024,128]{1,0:T(8,128)}, u32[]{:S(2)}) copy-start(f32[1024,128]{1,0:T(8,128)} %table_ref.1) | copy-start | bytes 1572868
  17.6 0.9 %copy-start.4 = (f32[2,128]{1,0:T(2,128)S(1)}, f32[2,128]{1,0:T(2,128)}, u32[]{:S(2)}) copy-start(f32[2,128]{1,0:T(2,128)} %gain_ref.3) | copy-start | bytes 3076
where the time goes:
time: 24.2 us; the launch traced here: 23.9 us
  starting transfers between devices  8.89 us (37%)
  Pallas kernels  7.67 us (32%)
  waiting for transfers between devices  5.56 us (23%)
  local copies, waits for them, and re-layouts  1.06 us (4%)
  between operations  0.75 us (3%)
    ppermute x3, starting transfers between devices, gathered(): got = lax.ppermute(held, axis, pairs)  8.24 us
    ppermute x3, waiting for transfers between devices, gathered(): got = lax.ppermute(held, axis, pairs)  5.54 us
    pallas_call x1, Pallas kernels, gathered(): pl.pallas_call(functools.partial(part_kernel, 2 * heads), out_shape=(shap...  4.38 us
    pallas_call x1, Pallas kernels, gathered(): pl.pallas_call(project_kernel, out_shape=jax.ShapeDtypeStruct((seqs // 2...  1.37 us
    pallas_call x2, Pallas kernels, gathered(): pl.pallas_call(functools.partial(weights_kernel, layer), out_shape=(jax.S...  1.07 us
    unnamed x12, local copies, waits for them, and re-layouts  1.06 us
    pallas_call x1, Pallas kernels, gathered(): pl.pallas_call(table_kernel, out_shape=(jax.ShapeDtypeStruct((outer_out.s...  0.84 us
    ppermute x3, starting transfers between devices, gathered(): peers.append(lax.ppermute(value, 'br', swap))  0.58 us
  transfers between devices with their start and end apart: 7, of which 3 were waited for; matrix products, arithmetic and copies ran while one was open for 0% of the time, Pallas kernels for 8%

commit v1 on v0

--- a/solution.py
+++ b/solution.py
@@ -253,7 +253,7 @@
 
 def part_kernel(
     heads, own_ref, peer_ref, live_ref, in_0, end_0, in_1, end_1, table_ref, out_ref, grad_ref,
-    mixed, keys, vals, lines, turn, many, more,
+    mixed, keys, vals, lines, turns, many, more,
 ):
     me = lax.axis_index(("row", "head"))
     first = lax.axis_index("br") == 0
@@ -271,7 +271,8 @@
         mine, other = own_ref[slot, start:stop, :], peer_ref[slot, start:stop, :]
         return jnp.where(first, other, mine) if flip else jnp.where(first, mine, other)
 
-    def transpose_rows(values):
+    def transpose_rows(values, at):
+        turn = turns.at[at]
         turn[...] = values
         return jnp.concatenate([turn[pl.ds(j, n, stride=n), :] for j in range(n)], axis=0)
 
@@ -332,8 +333,8 @@
         ]
         q = q * factor
         keys[layer], vals[layer] = k, v
-        lines[...] = bias
-        biases = [lines[pl.ds(kk, n, stride=n), :] + shift[kk] for kk in range(n)]
+        lines[layer] = bias
+        biases = [lines[layer, pl.ds(kk, n, stride=n), :] + shift[kk] for kk in range(n)]
         logits = head_sums(
             jnp.concatenate(
                 [block(q, i) * keys[layer, i * n + kk : i * n + kk + 1, :] for i in range(n) for kk in range(n)],
@@ -397,7 +398,7 @@
                 d_bias[kk] = d_logit if d_bias[kk] is None else d_bias[kk] + d_logit
             d_q.append(piece)
         d_q = jnp.concatenate(d_q, axis=0) * factor
-        d_bias = transpose_rows(jnp.concatenate(d_bias, axis=0) * (1.0 / size))
+        d_bias = transpose_rows(jnp.concatenate(d_bias, axis=0) * (1.0 / size), 5 + layer)
         d_all = jnp.concatenate([d_q, row_sums(many), row_sums(more), d_gate, d_bias], axis=1)
         d_hat = times_stacked_t(d_all, in_ref[layer][...])
         inner = d_hat - jnp.mean(d_hat, axis=-1, keepdims=True)
@@ -405,13 +406,13 @@
         return grad + inner * scale
 
     pair_two, saved_start = forward(0, pair_one)
-    turned, saved_end = forward(1, transpose_rows(pair_two))
-    turn[...] = turned
-    out_ref[0] = turn[pl.ds(me, n, stride=n), :]
-    grad = backward(1, transpose_rows(cot), saved_end)
-    grad = backward(0, transpose_rows(grad), saved_start)
-    turn[...] = grad
-    grad_ref[0] = turn[pl.ds(pl.multiple_of(me * n, SUBLANES), n), :]
+    turned, saved_end = forward(1, transpose_rows(pair_two, 0))
+    turns[3] = turned
+    out_ref[0] = turns[3, pl.ds(me, n, stride=n), :]
+    grad = backward(1, transpose_rows(cot, 1), saved_end)
+    grad = backward(0, transpose_rows(grad, 2), saved_start)
+    turns[4] = grad
+    grad_ref[0] = turns[4, pl.ds(pl.multiple_of(me * n, SUBLANES), n), :]
 
 
 def spec(space=pltpu.VMEM):
@@ -515,8 +516,8 @@
             pltpu.VMEM((n * OPC // LANES, n * OPC, LANES), F32),
             pltpu.VMEM((layers, square, inner), F32),
             pltpu.VMEM((layers, square, inner), F32),
-            pltpu.VMEM((square, inner), F32),
-            pltpu.VMEM((square, width), F32),
+            pltpu.VMEM((layers, square, inner), F32),
+            pltpu.VMEM((5 + layers, square, width), F32),
             pltpu.VMEM((square * n, inner), F32),
             pltpu.VMEM((square * n, inner), F32),
         ],

time: 24.2 us -> 24.2 us (level)
  no operation moved by 1% of the time
where the time goes in v1:
time: 24.2 us; the launch traced here: 23.9 us
  starting transfers between devices  8.89 us (37%)
  Pallas kernels  7.66 us (32%)
  waiting for transfers between devices  5.56 us (23%)
  local copies, waits for them, and re-layouts  1.06 us (4%)
  between operations  0.75 us (3%)
    ppermute x3, starting transfers between devices, gathered(): got = lax.ppermute(held, axis, pairs)  8.24 us
    ppermute x3, waiting for transfers between devices, gathered(): got = lax.ppermute(held, axis, pairs)  5.54 us
    pallas_call x1, Pallas kernels, gathered(): pl.pallas_call(functools.partial(part_kernel, 2 * heads), out_shape=(shap...  4.38 us
    pallas_call x1, Pallas kernels, gathered(): pl.pallas_call(project_kernel, out_shape=jax.ShapeDtypeStruct((seqs // 2...  1.37 us
    pallas_call x2, Pallas kernels, gathered(): pl.pallas_call(functools.partial(weights_kernel, layer), out_shape=(jax.S...  1.07 us
    unnamed x12, local copies, waits for them, and re-layouts  1.06 us
    pallas_call x1, Pallas kernels, gathered(): pl.pallas_call(table_kernel, out_shape=(jax.ShapeDtypeStruct((outer_out.s...  0.84 us
    ppermute x3, starting transfers between devices, gathered(): peers.append(lax.ppermute(value, 'br', swap))  0.58 us
  transfers between devices with their start and end apart: 7, of which 3 were waited for; matrix products, arithmetic and copies ran while one was open for 0% of the time, Pallas kernels for 8%

profile of v1, /device:TPU:0, one launch (start us, length us, event | category | flops | bytes accessed | tf_op | source)
XLA Modules:
  0.0 23.9 jit_solution(4570899077747489645)
XLA Ops:
  0.6 1.4 %project.1 = f32[24,128]{1,0:T(8,128)S(1)} custom-call(f32[16,1,256]{2,1,0:T(1,128)} %refs_0_.1, s32[1,32]{1,0:T(1,128)} %bitcast.14, f32[1,256]{1,0:T(1,128)} %bitcast.13, f32[64,256]{1,0:T(8,128)} %bitcast.12, f32[1,8,128]{2,1,0:T(8,128)} %refs_4_.1, f32[1,8,128]{2,1,0:T(8,128)} %refs_5_.1), custom_call_target="tpu_custom_call" | custom-call | tf_op jit(solution)/shard_map/project/pallas_call | solution.py:460
  2.0 3.0 %collective-permute-start = (f32[1,24,128]{2,1,0:T(8,128)S(1)}, f32[1,24,128]{2,1,0:T(8,128)S(1)}, u32[]{:S(2)}, u32[]{:S(2)}) collective-permute-start(f32[1,24,128]{2,1,0:T(8,128)S(1)} %bitcast.5), channel_id=1, source_target_pairs={{0,2},{2,0},{1,3},{3,1},{4,6},{6,4},{5,7},{7,5},{8,10},{10,8},{9,1... | collective-permute-start | bytes 36872 | tf_op jit(solution)/shard_map/ppermute | solution.py:506
  5.0 1.7 %collective-permute-done = f32[1,24,128]{2,1,0:T(8,128)S(1)} collective-permute-done((f32[1,24,128]{2,1,0:T(8,128)S(1)}, f32[1,24,128]{2,1,0:T(8,128)S(1)}, u32[]{:S(2)}, u32[]{:S(2)}) %collective-permute-start) | collective-permute-done | bytes 12320 | tf_op jit(solution)/shard_map/ppermute | solution.py:506
  6.7 2.1 %collective-permute-start.1 = (f32[2,24,128]{2,1,0:T(8,128)S(1)}, f32[2,24,128]{2,1,0:T(8,128)S(1)}, u32[]{:S(2)}, u32[]{:S(2)}) collective-permute-start(f32[2,24,128]{2,1,0:T(8,128)S(1)} %pad_maximum_fusion.2), channel_id=1, source_target_pairs={{0,4},{4,0},{8,12},{12,8},{1,5},{5,1},{9,13},{13,9},{2,6},{6,2},{1... | collective-permute-start | bytes 73736 | tf_op jit(solution)/shard_map/ppermute | solution.py:506
  8.8 0.0 collective-permute-start.4
  8.8 1.8 %collective-permute-done.1 = f32[2,24,128]{2,1,0:T(8,128)S(1)} collective-permute-done((f32[2,24,128]{2,1,0:T(8,128)S(1)}, f32[2,24,128]{2,1,0:T(8,128)S(1)}, u32[]{:S(2)}, u32[]{:S(2)}) %collective-permute-start.1) | collective-permute-done | bytes 24608 | tf_op jit(solution)/shard_map/ppermute | solution.py:506
  10.6 0.0 copy-start.2
  10.6 0.0 copy-start.3
  10.6 3.1 %collective-permute-start.2 = (f32[4,24,128]{2,1,0:T(8,128)S(1)}, f32[4,24,128]{2,1,0:T(8,128)S(1)}, u32[]{:S(2)}, u32[]{:S(2)}) collective-permute-start(f32[4,24,128]{2,1,0:T(8,128)S(1)} %pad_maximum_fusion.1), channel_id=1, source_target_pairs={{0,8},{4,12},{8,0},{12,4},{1,9},{5,13},{9,1},{13,5},{2,10},{6,14},... | collective-permute-start | bytes 147464 | tf_op jit(solution)/shard_map/ppermute | solution.py:506
  13.7 2.1 %collective-permute-done.2 = f32[4,24,128]{2,1,0:T(8,128)S(1)} collective-permute-done((f32[4,24,128]{2,1,0:T(8,128)S(1)}, f32[4,24,128]{2,1,0:T(8,128)S(1)}, u32[]{:S(2)}, u32[]{:S(2)}) %collective-permute-start.2) | collective-permute-done | bytes 49184 | tf_op jit(solution)/shard_map/ppermute | solution.py:506
  15.8 0.0 copy-start.5
  15.8 0.1 collective-permute-start.3
  15.9 0.0 copy-done.2
  15.9 0.5 %collective-permute-start.6 = (f32[2,2,32,128]{3,2,1,0:T(8,128)S(1)}, f32[2,2,32,128]{3,2,1,0:T(8,128)S(1)}, u32[]{:S(2)}, u32[]{:S(2)}) collective-permute-start(f32[2,2,32,128]{3,2,1,0:T(8,128)S(1)} %copy-done.2), channel_id=1, source_target_pairs={{0,1},{1,0},{2,3},{3,2},{4,5},{5,4},{6,7},{7,6},{8,9},{9,8},{10,11... | collective-permute-start | bytes 196616 | tf_op jit(solution)/shard_map/ppermute | solution.py:484
  16.4 0.0 copy-done.3
  16.4 0.0 copy-start
  16.4 0.1 collective-permute-start.5
  16.5 0.0 copy-done.5
  16.5 0.0 copy-start.1
  16.5 1.0 %copy-done.1 = f32[1024,128]{1,0:T(8,128)S(1)} copy-done((f32[1024,128]{1,0:T(8,128)S(1)}, f32[1024,128]{1,0:T(8,128)}, u32[]{:S(2)}) %copy-start.1) | copy-done | bytes 524312
  17.6 0.0 copy-start.4
  17.6 0.8 %table.1 = (bf16[1024,256]{1,0:T(8,128)(2,1)S(1)}, f32[8,128]{1,0:T(8,128)S(1)}) custom-call(f32[1024,128]{1,0:T(8,128)S(1)} %copy-done.1, s32[8]{0:T(128)S(1)} %copy-done.5), custom_call_target="tpu_custom_call" | custom-call | flops 4194304 | bytes 1048576 | tf_op jit(solution)/shard_map/table/pallas_call | solution.py:470
  18.4 0.0 collective-permute-done.5.peer_bias
  18.4 0.0 collective-permute-done.6.peer_out
  18.4 0.0 collective-permute-done.4.peer_in
  18.4 0.0 copy-done
  18.4 0.0 copy-done.4
  18.5 0.5 %shard_map.132 = (bf16[256,640]{1,0:T(8,128)(2,1)S(1)}, bf16[256,128]{1,0:T(8,128)(2,1)S(1)}) custom-call(f32[2,128]{1,0:T(2,128)S(1)} %copy-done.4, f32[2,128,2,128]{3,2,1,0:T(2,128)S(1)} %copy-done, f32[2,128,2,128]{3,2,1,0:T(2,128)S(1)} %collective-permute-done.4.peer_in, f32[2,2,128]{2,1,0:T(2,128)S(1)} %bitcast.10, ...), custom_call_target="tpu_custom_call" | custom-call | flops 4194304 | bytes 1048576 | tf_op jit(solution)/shard_map/pallas_call | solution.py:487
  19.0 0.5 %shard_map.131 = (bf16[256,640]{1,0:T(8,128)(2,1)S(1)}, bf16[256,128]{1,0:T(8,128)(2,1)S(1)}) custom-call(f32[2,128]{1,0:T(2,128)S(1)} %copy-done.4, f32[2,128,2,128]{3,2,1,0:T(2,128)S(1)} %copy-done, f32[2,128,2,128]{3,2,1,0:T(2,128)S(1)} %collective-permute-done.4.peer_in, f32[2,2,128]{2,1,0:T(2,128)S(1)} %bitcast.11, ...), custom_call_target="tpu_custom_call" | custom-call | flops 4194304 | bytes 1048576 | tf_op jit(solution)/shard_map/pallas_call | solution.py:487
  19.5 0.0 collective-permute-done.3.peer_ref
  19.6 4.4 %part.1 = (f32[1,8,128]{2,1,0:T(8,128)}, f32[1,8,128]{2,1,0:T(8,128)}) custom-call(f32[8,24,128]{2,1,0:T(8,128)S(1)} %pad_maximum_fusion.own_ref, f32[8,24,128]{2,1,0:T(8,128)S(1)} %collective-permute-done.3.peer_ref, f32[8,128]{1,0:T(8,128)S(1)} %get-tuple-element.8.live_ref, bf16[256,640]{1,0:T(8,128)(2,1)S(1)} %get-tuple-element.9.in_0, ...), custom_call_target="tpu_custom_call" | custom-call | tf_op jit(solution)/shard_map/part/pallas_call | solution.py:510
  (3 shorter events, 0.0 us)
Async XLA Ops:
  2.0 4.7 %collective-permute-start = (f32[1,24,128]{2,1,0:T(8,128)S(1)}, f32[1,24,128]{2,1,0:T(8,128)S(1)}, u32[]{:S(2)}, u32[]{:S(2)}) collective-permute-start(f32[1,24,128]{2,1,0:T(8,128)S(1)} %bitcast.5), channel_id=1, source_target_pairs={{0,2},{2,0},{1,3},{3,1},{4,6},{6,4},{5,7},{7,5},{8,10},{10,8},{9,1... | collective-permute-start | bytes 36872 | tf_op jit(solution)/shard_map/ppermute | solution.py:506
  6.7 3.9 %collective-permute-start.1 = (f32[2,24,128]{2,1,0:T(8,128)S(1)}, f32[2,24,128]{2,1,0:T(8,128)S(1)}, u32[]{:S(2)}, u32[]{:S(2)}) collective-permute-start(f32[2,24,128]{2,1,0:T(8,128)S(1)} %pad_maximum_fusion.2), channel_id=1, source_target_pairs={{0,4},{4,0},{8,12},{12,8},{1,5},{5,1},{9,13},{13,9},{2,6},{6,2},{1... | collective-permute-start | bytes 73736 | tf_op jit(solution)/shard_map/ppermute | solution.py:506
  8.8 9.6 %collective-permute-start.4 = (f32[2,128,2,128]{3,2,1,0:T(2,128)}, f32[2,128,2,128]{3,2,1,0:T(2,128)S(1)}, u32[]{:S(2)}, u32[]{:S(2)}) collective-permute-start(f32[2,128,2,128]{3,2,1,0:T(2,128)} %own_in.3), channel_id=1, source_target_pairs={{0,1},{1,0},{2,3},{3,2},{4,5},{5,4},{6,7},{7,6},{8,9},{9,8},{10,11... | collective-permute-start | bytes 786440 | tf_op jit(solution)/shard_map/ppermute | solution.py:484
  10.6 5.3 %copy-start.2 = (f32[2,2,32,128]{3,2,1,0:T(8,128)S(1)}, f32[2,2,32,128]{3,2,1,0:T(8,128)}, u32[]{:S(2)}) copy-start(f32[2,2,32,128]{3,2,1,0:T(8,128)} %own_out.3) | copy-start | bytes 196612
  10.6 5.8 %copy-start.3 = (f32[2,128,2]{1,2,0:T(2,128)S(1)}, f32[2,128,2]{1,2,0:T(2,128)}, u32[]{:S(2)}) copy-start(f32[2,128,2]{1,2,0:T(2,128)} %param.21) | copy-start | bytes 6148
  10.6 5.2 %collective-permute-start.2 = (f32[4,24,128]{2,1,0:T(8,128)S(1)}, f32[4,24,128]{2,1,0:T(8,128)S(1)}, u32[]{:S(2)}, u32[]{:S(2)}) collective-permute-start(f32[4,24,128]{2,1,0:T(8,128)S(1)} %pad_maximum_fusion.1), channel_id=1, source_target_pairs={{0,8},{4,12},{8,0},{12,4},{1,9},{5,13},{9,1},{13,5},{2,10},{6,14},... | collective-permute-start | bytes 147464 | tf_op jit(solution)/shard_map/ppermute | solution.py:506
  15.8 0.7 %copy-start.5 = (s32[8]{0:T(128)S(1)}, s32[8]{0:T(128)}, u32[]{:S(2)}) copy-start(s32[8]{0:T(128)} %live_ref.1) | copy-start | bytes 100
  15.8 3.7 %collective-permute-start.3 = (f32[8,24,128]{2,1,0:T(8,128)S(1)}, f32[8,24,128]{2,1,0:T(8,128)S(1)}, u32[]{:S(2)}, u32[]{:S(2)}) collective-permute-start(f32[8,24,128]{2,1,0:T(8,128)S(1)} %pad_maximum_fusion.own_ref), channel_id=1, source_target_pairs={{0,1},{1,0},{2,3},{3,2},{4,5},{5,4},{6,7},{7,6},{8,9},{9,8},{10,11... | collective-permute-start | bytes 294920 | tf_op jit(solution)/shard_map/ppermute | solution.py:508
  15.9 2.5 %collective-permute-start.6 = (f32[2,2,32,128]{3,2,1,0:T(8,128)S(1)}, f32[2,2,32,128]{3,2,1,0:T(8,128)S(1)}, u32[]{:S(2)}, u32[]{:S(2)}) collective-permute-start(f32[2,2,32,128]{3,2,1,0:T(8,128)S(1)} %copy-done.2), channel_id=1, source_target_pairs={{0,1},{1,0},{2,3},{3,2},{4,5},{5,4},{6,7},{7,6},{8,9},{9,8},{10,11... | collective-permute-start | bytes 196616 | tf_op jit(solution)/shard_map/ppermute | solution.py:484
  16.4 2.0 %copy-start = (f32[2,128,2,128]{3,2,1,0:T(2,128)S(1)}, f32[2,128,2,128]{3,2,1,0:T(2,128)}, u32[]{:S(2)}) copy-start(f32[2,128,2,128]{3,2,1,0:T(2,128)} %own_in.3) | copy-start | bytes 786436
  16.4 2.0 %collective-permute-start.5 = (f32[2,2,128]{2,1,0:T(2,128)S(1)}, f32[2,2,128]{2,1,0:T(2,128)S(1)}, u32[]{:S(2)}, u32[]{:S(2)}) collective-permute-start(f32[2,2,128]{2,1,0:T(2,128)S(1)} %bitcast.9), channel_id=1, source_target_pairs={{0,1},{1,0},{2,3},{3,2},{4,5},{5,4},{6,7},{7,6},{8,9},{9,8},{10,11... | collective-permute-start | bytes 6152 | tf_op jit(solution)/shard_map/ppermute | solution.py:484
  16.5 1.0 %copy-start.1 = (f32[1024,128]{1,0:T(8,128)S(1)}, f32[1024,128]{1,0:T(8,128)}, u32[]{:S(2)}) copy-start(f32[1024,128]{1,0:T(8,128)} %table_ref.1) | copy-start | bytes 1572868
  17.6 0.9 %copy-start.4 = (f32[2,128]{1,0:T(2,128)S(1)}, f32[2,128]{1,0:T(2,128)}, u32[]{:S(2)}) copy-start(f32[2,128]{1,0:T(2,128)} %gain_ref.3) | copy-start | bytes 3076

commit v2 on v1

--- a/solution.py
+++ b/solution.py
@@ -256,8 +256,11 @@
     mixed, keys, vals, lines, turns, many, more,
 ):
     me = lax.axis_index(("row", "head"))
-    first = lax.axis_index("br") == 0
     n = own_ref.shape[0]
+    bits = bits_of(n)
+    mine_at = reverse(me, bits)
+    part = lax.axis_index("br") ^ parity(me, bits)
+    straight = (part == 0, part == 1)
     count = n
     rows = own_ref.shape[1] - count - SUBLANES
     total = n * n
@@ -267,9 +270,10 @@
     size = heads_wide // heads
 
     def taken(start, stop, r, flip):
-        slot = jnp.bitwise_xor(me, r)
+        slot = mine_at ^ reverse(r, bits)
         mine, other = own_ref[slot, start:stop, :], peer_ref[slot, start:stop, :]
-        return jnp.where(first, other, mine) if flip else jnp.where(first, mine, other)
+        pick = straight[parity(r, bits)]
+        return jnp.where(pick, other, mine) if flip else jnp.where(pick, mine, other)
 
     def transpose_rows(values, at):
         turn = turns.at[at]
@@ -296,16 +300,16 @@
     )
     per = LANES // OPC
     chunks = []
-    for part in range(n // per):
-        mixed[part] = product[:, part * LANES : (part + 1) * LANES]
+    for piece in range(n // per):
+        mixed[piece] = product[:, piece * LANES : (piece + 1) * LANES]
         lots = []
         for base in range(0, OPC, per):
-            lots.append(regroup([mixed[part, pl.ds(base + g, n, stride=OPC), :] for g in range(per)], OPC))
+            lots.append(regroup([mixed[piece, pl.ds(base + g, n, stride=OPC), :] for g in range(per)], OPC))
         chunks += [[lot[g] for lot in lots] for g in range(per)]
     spread = jnp.concatenate([jnp.concatenate(c, axis=1) for c in chunks], axis=0)
     outer = times_beside(spread, table_ref[...])
     seen = jnp.concatenate(
-        [own_ref[jnp.bitwise_xor(me, r), rows + count : rows + count + 1, :] for r in range(n)], axis=0
+        [own_ref[mine_at ^ reverse(r, bits), rows + count : rows + count + 1, :] for r in range(n)], axis=0
     )
     both = jnp.concatenate([seen * seen[i : i + 1] for i in range(n)], axis=0)
     counts = dot(both.astype(BF16), jnp.ones((LANES, width), BF16))
@@ -425,6 +429,24 @@
 
 def limit(mebibytes):
     return pltpu.CompilerParams(vmem_limit_bytes=mebibytes << 20)
+
+
+def bits_of(count):
+    return count.bit_length() - 1
+
+
+def reverse(index, bits):
+    back = 0
+    for k in range(bits):
+        back = back | (((index >> k) & 1) << (bits - 1 - k))
+    return back
+
+
+def parity(index, bits):
+    odd = 0
+    for k in range(bits):
+        odd = odd ^ ((index >> k) & 1)
+    return odd
 
 
 def opposite(count, bit):
@@ -496,14 +518,9 @@
             cost_estimate=cost(1 << 22),
         )(tri_gain, tri_in, peers[0], bias, peers[1], tri_out, peers[2])
     held = payload[None]
-    steps = []
-    for axis in ("head", "row"):
-        bit = 1
-        while bit < lax.axis_size(axis):
-            steps.append((axis, opposite(lax.axis_size(axis), bit)))
-            bit *= 2
-    for axis, pairs in steps:
-        got = lax.ppermute(held, axis, pairs)
+    for at in range(bits_of(n)):
+        pairs = opposite(2 * n, (n >> at) | 1)
+        got = lax.ppermute(held, ("row", "head", "br"), pairs)
         held = jnp.concatenate([held, got], axis=0)
     other = lax.ppermute(held, "br", swap)
     shape = jax.ShapeDtypeStruct((1, n, width), F32)

time: 24.2 us -> 22.8 us (0.942)
  waiting for transfers between devices: 5.56 us -> 4.41 us
  starting transfers between devices: 8.89 us -> 8.64 us
    ppermute x3, waiting for transfers between devices: 5.54 us -> 4.4 us  [gathered(): got = lax.ppermute(held, ('row', 'head', 'br'), pairs)]
    ppermute x3, starting transfers between devices: 8.24 us -> 7.16 us  [gathered(): got = lax.ppermute(held, ('row', 'head', 'br'), pairs)]
    ppermute x1, starting transfers between devices: 0.07 us -> 0.57 us  [gathered(): other = lax.ppermute(held, 'br', swap)]
    ppermute x3, starting transfers between devices: 0.58 us -> 0.91 us  [gathered(): peers.append(lax.ppermute(value, 'br', swap))]
where the time goes in v2:
time: 22.8 us; the launch traced here: 22.5 us
  starting transfers between devices  8.64 us (38%)
  Pallas kernels  7.67 us (34%)
  waiting for transfers between devices  4.41 us (19%)
  local copies, waits for them, and re-layouts  1.06 us (5%)
  between operations  0.73 us (3%)
    ppermute x3, starting transfers between devices, gathered(): got = lax.ppermute(held, ('row', 'head', 'br'), pairs)  7.16 us
    ppermute x3, waiting for transfers between devices, gathered(): got = lax.ppermute(held, ('row', 'head', 'br'), pairs)  4.4 us
    pallas_call x1, Pallas kernels, gathered(): pl.pallas_call(functools.partial(part_kernel, 2 * heads), out_shape=(shap...  4.39 us
    pallas_call x1, Pallas kernels, gathered(): pl.pallas_call(project_kernel, out_shape=jax.ShapeDtypeStruct((seqs // 2...  1.37 us
    pallas_call x2, Pallas kernels, gathered(): pl.pallas_call(functools.partial(weights_kernel, layer), out_shape=(jax.S...  1.07 us
    unnamed x12, local copies, waits for them, and re-layouts  1.06 us
    ppermute x3, starting transfers between devices, gathered(): peers.append(lax.ppermute(value, 'br', swap))  0.91 us
    pallas_call x1, Pallas kernels, gathered(): pl.pallas_call(table_kernel, out_shape=(jax.ShapeDtypeStruct((outer_out.s...  0.84 us
  transfers between devices with their start and end apart: 7, of which 3 were waited for; matrix products, arithmetic and copies ran while one was open for 0% of the time, Pallas kernels for 8%

profile of v2, /device:TPU:0, one launch (start us, length us, event | category | flops | bytes accessed | tf_op | source)
XLA Modules:
  0.0 22.5 jit_solution(2271981299900464994)
XLA Ops:
  0.6 1.4 %project.1 = f32[24,128]{1,0:T(8,128)S(1)} custom-call(f32[16,1,256]{2,1,0:T(1,128)} %refs_0_.1, s32[1,32]{1,0:T(1,128)} %bitcast.14, f32[1,256]{1,0:T(1,128)} %bitcast.13, f32[64,256]{1,0:T(8,128)} %bitcast.12, f32[1,8,128]{2,1,0:T(8,128)} %refs_4_.1, f32[1,8,128]{2,1,0:T(8,128)} %refs_5_.1), custom_call_target="tpu_custom_call" | custom-call | tf_op jit(solution)/shard_map/project/pallas_call | solution.py:482
  2.0 3.6 %collective-permute-start = (f32[1,24,128]{2,1,0:T(8,128)S(1)}, f32[1,24,128]{2,1,0:T(8,128)S(1)}, u32[]{:S(2)}, u32[]{:S(2)}) collective-permute-start(f32[1,24,128]{2,1,0:T(8,128)S(1)} %bitcast.5), channel_id=1, source_target_pairs={{0,9},{1,8},{2,11},{3,10},{4,13},{5,12},{6,15},{7,14},{8,1},{9,0},... | collective-permute-start | bytes 36872 | tf_op jit(solution)/shard_map/ppermute | solution.py:523
  5.6 1.4 %collective-permute-done = f32[1,24,128]{2,1,0:T(8,128)S(1)} collective-permute-done((f32[1,24,128]{2,1,0:T(8,128)S(1)}, f32[1,24,128]{2,1,0:T(8,128)S(1)}, u32[]{:S(2)}, u32[]{:S(2)}) %collective-permute-start) | collective-permute-done | bytes 12320 | tf_op jit(solution)/shard_map/ppermute | solution.py:523
  7.0 1.9 %collective-permute-start.1 = (f32[2,24,128]{2,1,0:T(8,128)S(1)}, f32[2,24,128]{2,1,0:T(8,128)S(1)}, u32[]{:S(2)}, u32[]{:S(2)}) collective-permute-start(f32[2,24,128]{2,1,0:T(8,128)S(1)} %pad_maximum_fusion.2), channel_id=1, source_target_pairs={{0,5},{1,4},{2,7},{3,6},{4,1},{5,0},{6,3},{7,2},{8,13},{9,12},{10,... | collective-permute-start | bytes 73736 | tf_op jit(solution)/shard_map/ppermute | solution.py:523
  8.9 0.4 %collective-permute-start.4 = (f32[2,128,2,128]{3,2,1,0:T(2,128)}, f32[2,128,2,128]{3,2,1,0:T(2,128)S(1)}, u32[]{:S(2)}, u32[]{:S(2)}) collective-permute-start(f32[2,128,2,128]{3,2,1,0:T(2,128)} %own_in.3), channel_id=1, source_target_pairs={{0,1},{1,0},{2,3},{3,2},{4,5},{5,4},{6,7},{7,6},{8,9},{9,8},{10,11... | collective-permute-start | bytes 786440 | tf_op jit(solution)/shard_map/ppermute | solution.py:506
  9.3 1.1 %collective-permute-done.1 = f32[2,24,128]{2,1,0:T(8,128)S(1)} collective-permute-done((f32[2,24,128]{2,1,0:T(8,128)S(1)}, f32[2,24,128]{2,1,0:T(8,128)S(1)}, u32[]{:S(2)}, u32[]{:S(2)}) %collective-permute-start.1) | collective-permute-done | bytes 24608 | tf_op jit(solution)/shard_map/ppermute | solution.py:523
  10.4 0.0 copy-start.2
  10.4 0.0 copy-start.3
  10.4 1.7 %collective-permute-start.2 = (f32[4,24,128]{2,1,0:T(8,128)S(1)}, f32[4,24,128]{2,1,0:T(8,128)S(1)}, u32[]{:S(2)}, u32[]{:S(2)}) collective-permute-start(f32[4,24,128]{2,1,0:T(8,128)S(1)} %pad_maximum_fusion.1), channel_id=1, source_target_pairs={{0,3},{1,2},{2,1},{3,0},{4,7},{5,6},{6,5},{7,4},{8,11},{9,10},{10,... | collective-permute-start | bytes 147464 | tf_op jit(solution)/shard_map/ppermute | solution.py:523
  12.1 1.9 %collective-permute-done.2 = f32[4,24,128]{2,1,0:T(8,128)S(1)} collective-permute-done((f32[4,24,128]{2,1,0:T(8,128)S(1)}, f32[4,24,128]{2,1,0:T(8,128)S(1)}, u32[]{:S(2)}, u32[]{:S(2)}) %collective-permute-start.2) | collective-permute-done | bytes 49184 | tf_op jit(solution)/shard_map/ppermute | solution.py:523
  14.0 0.0 copy-start.5
  14.0 0.6 %collective-permute-start.3 = (f32[8,24,128]{2,1,0:T(8,128)S(1)}, f32[8,24,128]{2,1,0:T(8,128)S(1)}, u32[]{:S(2)}, u32[]{:S(2)}) collective-permute-start(f32[8,24,128]{2,1,0:T(8,128)S(1)} %pad_maximum_fusion.own_ref), channel_id=1, source_target_pairs={{0,1},{1,0},{2,3},{3,2},{4,5},{5,4},{6,7},{7,6},{8,9},{9,8},{10,11... | collective-permute-start | bytes 294920 | tf_op jit(solution)/shard_map/ppermute | solution.py:525
  14.6 0.0 copy-done.2
  14.6 0.1 collective-permute-start.6
  14.7 0.0 copy-done.3
  14.7 0.0 copy-start
  14.7 0.4 %collective-permute-start.5 = (f32[2,2,128]{2,1,0:T(2,128)S(1)}, f32[2,2,128]{2,1,0:T(2,128)S(1)}, u32[]{:S(2)}, u32[]{:S(2)}) collective-permute-start(f32[2,2,128]{2,1,0:T(2,128)S(1)} %bitcast.9), channel_id=1, source_target_pairs={{0,1},{1,0},{2,3},{3,2},{4,5},{5,4},{6,7},{7,6},{8,9},{9,8},{10,11... | collective-permute-start | bytes 6152 | tf_op jit(solution)/shard_map/ppermute | solution.py:506
  15.1 0.0 copy-done.5
  15.1 0.0 copy-start.1
  15.1 1.0 %copy-done.1 = f32[1024,128]{1,0:T(8,128)S(1)} copy-done((f32[1024,128]{1,0:T(8,128)S(1)}, f32[1024,128]{1,0:T(8,128)}, u32[]{:S(2)}) %copy-start.1) | copy-done | bytes 524312
  16.1 0.0 copy-start.4
  16.1 0.8 %table.1 = (bf16[1024,256]{1,0:T(8,128)(2,1)S(1)}, f32[8,128]{1,0:T(8,128)S(1)}) custom-call(f32[1024,128]{1,0:T(8,128)S(1)} %copy-done.1, s32[8]{0:T(128)S(1)} %copy-done.5), custom_call_target="tpu_custom_call" | custom-call | flops 4194304 | bytes 1048576 | tf_op jit(solution)/shard_map/table/pallas_call | solution.py:492
  17.0 0.0 collective-permute-done.5.peer_bias
  17.0 0.0 collective-permute-done.6.peer_out
  17.0 0.0 collective-permute-done.4.peer_in
  17.0 0.0 copy-done
  17.0 0.0 copy-done.4
  17.0 0.5 %shard_map.132 = (bf16[256,640]{1,0:T(8,128)(2,1)S(1)}, bf16[256,128]{1,0:T(8,128)(2,1)S(1)}) custom-call(f32[2,128]{1,0:T(2,128)S(1)} %copy-done.4, f32[2,128,2,128]{3,2,1,0:T(2,128)S(1)} %copy-done, f32[2,128,2,128]{3,2,1,0:T(2,128)S(1)} %collective-permute-done.4.peer_in, f32[2,2,128]{2,1,0:T(2,128)S(1)} %bitcast.10, ...), custom_call_target="tpu_custom_call" | custom-call | flops 4194304 | bytes 1048576 | tf_op jit(solution)/shard_map/pallas_call | solution.py:509
  17.6 0.5 %shard_map.131 = (bf16[256,640]{1,0:T(8,128)(2,1)S(1)}, bf16[256,128]{1,0:T(8,128)(2,1)S(1)}) custom-call(f32[2,128]{1,0:T(2,128)S(1)} %copy-done.4, f32[2,128,2,128]{3,2,1,0:T(2,128)S(1)} %copy-done, f32[2,128,2,128]{3,2,1,0:T(2,128)S(1)} %collective-permute-done.4.peer_in, f32[2,2,128]{2,1,0:T(2,128)S(1)} %bitcast.11, ...), custom_call_target="tpu_custom_call" | custom-call | flops 4194304 | bytes 1048576 | tf_op jit(solution)/shard_map/pallas_call | solution.py:509
  18.1 0.0 collective-permute-done.3.peer_ref
  18.1 4.4 %part.1 = (f32[1,8,128]{2,1,0:T(8,128)}, f32[1,8,128]{2,1,0:T(8,128)}) custom-call(f32[8,24,128]{2,1,0:T(8,128)S(1)} %pad_maximum_fusion.own_ref, f32[8,24,128]{2,1,0:T(8,128)S(1)} %collective-permute-done.3.peer_ref, f32[8,128]{1,0:T(8,128)S(1)} %get-tuple-element.8.live_ref, bf16[256,640]{1,0:T(8,128)(2,1)S(1)} %get-tuple-element.9.in_0, ...), custom_call_target="tpu_custom_call" | custom-call | tf_op jit(solution)/shard_map/part/pallas_call | solution.py:527
  (3 shorter events, 0.0 us)
Async XLA Ops:
  2.0 5.0 %collective-permute-start = (f32[1,24,128]{2,1,0:T(8,128)S(1)}, f32[1,24,128]{2,1,0:T(8,128)S(1)}, u32[]{:S(2)}, u32[]{:S(2)}) collective-permute-start(f32[1,24,128]{2,1,0:T(8,128)S(1)} %bitcast.5), channel_id=1, source_target_pairs={{0,9},{1,8},{2,11},{3,10},{4,13},{5,12},{6,15},{7,14},{8,1},{9,0},... | collective-permute-start | bytes 36872 | tf_op jit(solution)/shard_map/ppermute | solution.py:523
  7.0 3.4 %collective-permute-start.1 = (f32[2,24,128]{2,1,0:T(8,128)S(1)}, f32[2,24,128]{2,1,0:T(8,128)S(1)}, u32[]{:S(2)}, u32[]{:S(2)}) collective-permute-start(f32[2,24,128]{2,1,0:T(8,128)S(1)} %pad_maximum_fusion.2), channel_id=1, source_target_pairs={{0,5},{1,4},{2,7},{3,6},{4,1},{5,0},{6,3},{7,2},{8,13},{9,12},{10,... | collective-permute-start | bytes 73736 | tf_op jit(solution)/shard_map/ppermute | solution.py:523
  8.9 8.1 %collective-permute-start.4 = (f32[2,128,2,128]{3,2,1,0:T(2,128)}, f32[2,128,2,128]{3,2,1,0:T(2,128)S(1)}, u32[]{:S(2)}, u32[]{:S(2)}) collective-permute-start(f32[2,128,2,128]{3,2,1,0:T(2,128)} %own_in.3), channel_id=1, source_target_pairs={{0,1},{1,0},{2,3},{3,2},{4,5},{5,4},{6,7},{7,6},{8,9},{9,8},{10,11... | collective-permute-start | bytes 786440 | tf_op jit(solution)/shard_map/ppermute | solution.py:506
  10.4 4.2 %copy-start.2 = (f32[2,2,32,128]{3,2,1,0:T(8,128)S(1)}, f32[2,2,32,128]{3,2,1,0:T(8,128)}, u32[]{:S(2)}) copy-start(f32[2,2,32,128]{3,2,1,0:T(8,128)} %own_out.3) | copy-start | bytes 196612
  10.4 4.3 %copy-start.3 = (f32[2,128,2]{1,2,0:T(2,128)S(1)}, f32[2,128,2]{1,2,0:T(2,128)}, u32[]{:S(2)}) copy-start(f32[2,128,2]{1,2,0:T(2,128)} %param.21) | copy-start | bytes 6148
  10.4 3.6 %collective-permute-start.2 = (f32[4,24,128]{2,1,0:T(8,128)S(1)}, f32[4,24,128]{2,1,0:T(8,128)S(1)}, u32[]{:S(2)}, u32[]{:S(2)}) collective-permute-start(f32[4,24,128]{2,1,0:T(8,128)S(1)} %pad_maximum_fusion.1), channel_id=1, source_target_pairs={{0,3},{1,2},{2,1},{3,0},{4,7},{5,6},{6,5},{7,4},{8,11},{9,10},{10,... | collective-permute-start | bytes 147464 | tf_op jit(solution)/shard_map/ppermute | solution.py:523
  14.0 1.1 %copy-start.5 = (s32[8]{0:T(128)S(1)}, s32[8]{0:T(128)}, u32[]{:S(2)}) copy-start(s32[8]{0:T(128)} %live_ref.1) | copy-start | bytes 100
  14.0 4.1 %collective-permute-start.3 = (f32[8,24,128]{2,1,0:T(8,128)S(1)}, f32[8,24,128]{2,1,0:T(8,128)S(1)}, u32[]{:S(2)}, u32[]{:S(2)}) collective-permute-start(f32[8,24,128]{2,1,0:T(8,128)S(1)} %pad_maximum_fusion.own_ref), channel_id=1, source_target_pairs={{0,1},{1,0},{2,3},{3,2},{4,5},{5,4},{6,7},{7,6},{8,9},{9,8},{10,11... | collective-permute-start | bytes 294920 | tf_op jit(solution)/shard_map/ppermute | solution.py:525
  14.6 2.4 %collective-permute-start.6 = (f32[2,2,32,128]{3,2,1,0:T(8,128)S(1)}, f32[2,2,32,128]{3,2,1,0:T(8,128)S(1)}, u32[]{:S(2)}, u32[]{:S(2)}) collective-permute-start(f32[2,2,32,128]{3,2,1,0:T(8,128)S(1)} %copy-done.2), channel_id=1, source_target_pairs={{0,1},{1,0},{2,3},{3,2},{4,5},{5,4},{6,7},{7,6},{8,9},{9,8},{10,11... | collective-permute-start | bytes 196616 | tf_op jit(solution)/shard_map/ppermute | solution.py:506
  14.7 2.4 %copy-start = (f32[2,128,2,128]{3,2,1,0:T(2,128)S(1)}, f32[2,128,2,128]{3,2,1,0:T(2,128)}, u32[]{:S(2)}) copy-start(f32[2,128,2,128]{3,2,1,0:T(2,128)} %own_in.3) | copy-start | bytes 786436
  14.7 2.3 %collective-permute-start.5 = (f32[2,2,128]{2,1,0:T(2,128)S(1)}, f32[2,2,128]{2,1,0:T(2,128)S(1)}, u32[]{:S(2)}, u32[]{:S(2)}) collective-permute-start(f32[2,2,128]{2,1,0:T(2,128)S(1)} %bitcast.9), channel_id=1, source_target_pairs={{0,1},{1,0},{2,3},{3,2},{4,5},{5,4},{6,7},{7,6},{8,9},{9,8},{10,11... | collective-permute-start | bytes 6152 | tf_op jit(solution)/shard_map/ppermute | solution.py:506
  15.1 1.0 %copy-start.1 = (f32[1024,128]{1,0:T(8,128)S(1)}, f32[1024,128]{1,0:T(8,128)}, u32[]{:S(2)}) copy-start(f32[1024,128]{1,0:T(8,128)} %table_ref.1) | copy-start | bytes 1572868
  16.1 0.9 %copy-start.4 = (f32[2,128]{1,0:T(2,128)S(1)}, f32[2,128]{1,0:T(2,128)}, u32[]{:S(2)}) copy-start(f32[2,128]{1,0:T(2,128)} %gain_ref.3) | copy-start | bytes 3076

commit v3 on v2

--- a/solution.py
+++ b/solution.py
@@ -196,29 +196,30 @@
     ]
     for copy in copies:
         copy.start()
-    for copy in copies:
-        copy.wait()
-    project_part(*held, out_ref)
-
-
-def project_part(align_ref, mask_ref, gain_ref, proj_ref, pair_ref, cot_ref, out_ref):
+    align_ref, proj_ref, gain_ref, mask_ref, pair_ref, cot_ref = held
     part = lax.axis_index("br")
     seqs, _, width = align_ref.shape
     rows = seqs // 2
+    copies[0].wait()
+    normed, _ = centre(jnp.reshape(align_ref[...], (seqs, width)))
+    copies[1].wait()
+    stacked = jnp.concatenate(split2(proj_ref[...]), axis=0)
+    copies[2].wait()
+    projected = times_stacked_t(normed * gain_ref[...], stacked)
+    copies[3].wait()
     line = mask_ref[...].astype(F32)
     sequence = lax.broadcasted_iota(jnp.int32, (seqs, line.shape[1]), 0) + part * seqs
     lane = lax.broadcasted_iota(jnp.int32, (seqs, line.shape[1]), 1)
     own = jnp.sum(jnp.where(sequence == lane, line, 0.0), axis=1, keepdims=True)
-    values = jnp.reshape(align_ref[...], (seqs, width))
-    normed, _ = centre(values)
-    stacked = jnp.concatenate(split2(proj_ref[...]), axis=0)
-    projected = times_stacked_t(normed * gain_ref[...], stacked) * own
-    out_ref[0:rows, :] = jnp.concatenate([projected[:rows], projected[rows:]], axis=1)
-    count = pair_ref.shape[1]
-    out_ref[rows : rows + count, :] = jnp.where(part == 0, pair_ref[0], cot_ref[0])
     rest = jnp.zeros((1, LANES - line.shape[1]), F32)
     line = jnp.concatenate([line, rest], axis=1)
+    count = pair_ref.shape[1]
     out_ref[rows + count :, :] = jnp.broadcast_to(line, (SUBLANES, LANES))
+    copies[4].wait()
+    copies[5].wait()
+    out_ref[rows : rows + count, :] = jnp.where(part == 0, pair_ref[0], cot_ref[0])
+    projected = projected * own
+    out_ref[0:rows, :] = jnp.concatenate([projected[:rows], projected[rows:]], axis=1)
 
 
 def weights_kernel(layer, gain_ref, own_in, peer_in, own_bias, peer_bias, own_out, peer_out, in_ref, out_ref):
@@ -329,12 +330,14 @@
     def block(values, i):
         return values[i * n : (i + 1) * n]
 
-    def forward(layer, entry):
+    def forward(layer, entry, own_entry=None):
         hat, scale = centre(entry)
-        projected = times_stacked(hat, in_ref[layer][...])
-        q, k, v, gate, bias = [
-            projected[:, t * heads_wide : (t + 1) * heads_wide] for t in range(5)
-        ]
+        wide = 2 * heads_wide
+        pair_qk = times_stacked(hat, in_ref[layer][:, :wide])
+        pair_vg = times_stacked(hat, in_ref[layer][:, wide : 2 * wide])
+        bias = times_stacked(hat, in_ref[layer][:, 2 * wide :])
+        q, k = pair_qk[:, :heads_wide], pair_qk[:, heads_wide:]
+        v, gate = pair_vg[:, :heads_wide], pair_vg[:, heads_wide:]
         q = q * factor
         keys[layer], vals[layer] = k, v
         lines[layer] = bias
@@ -364,16 +367,25 @@
             attended.append(mix)
         attended = jnp.concatenate(attended, axis=0)
         opened = jax.nn.sigmoid(gate)
-        update = times_stacked(opened * attended, end_ref[layer][...])
-        return entry + update * pair_mask, (hat, scale, q, opened, attended, probs)
-
-    def row_sums(scratch):
-        whole = scratch[pl.ds(0, total, stride=n), :]
+        gated, mask = opened * attended, pair_mask
+        if own_entry is not None:
+            turns[3] = gated
+            gated, entry = turns[3, pl.ds(me, n, stride=n), :], own_entry
+            mask = live * live_ref[pl.ds(me, 1), :]
+        update = times_stacked(gated, end_ref[layer][...])
+        return entry + update * mask, (hat, scale, q, opened, attended, probs)
+
+    def row_sums(scratch, start, size):
+        whole = scratch[pl.ds(start, size, stride=n), :]
         for j in range(1, n):
-            whole = whole + scratch[pl.ds(j, total, stride=n), :]
+            whole = whole + scratch[pl.ds(start + j, size, stride=n), :]
         return whole
 
-    def backward(layer, grad, saved):
+    def own_rows(values, at):
+        turns[at] = values
+        return turns[at, pl.ds(pl.multiple_of(me * n, SUBLANES), n), :]
+
+    def backward(layer, grad, saved, own_only):
         hat, scale, q, opened, attended, probs = saved
         pulled = times_stacked_t(grad * pair_mask, end_ref[layer][...])
         d_att = pulled * opened
@@ -402,21 +414,32 @@
                 d_bias[kk] = d_logit if d_bias[kk] is None else d_bias[kk] + d_logit
             d_q.append(piece)
         d_q = jnp.concatenate(d_q, axis=0) * factor
-        d_bias = transpose_rows(jnp.concatenate(d_bias, axis=0) * (1.0 / size), 5 + layer)
-        d_all = jnp.concatenate([d_q, row_sums(many), row_sums(more), d_gate, d_bias], axis=1)
-        d_hat = times_stacked_t(d_all, in_ref[layer][...])
+        d_bias = jnp.concatenate(d_bias, axis=0) * (1.0 / size)
+        start, rows_wanted = 0, total
+        if own_only:
+            turns[5 + layer] = d_bias
+            d_bias = turns[5 + layer, pl.ds(me, n, stride=n), :]
+            start, rows_wanted = me * n * n, n
+            d_q, d_gate = own_rows(d_q, 4), own_rows(d_gate, 7)
+            hat, grad = own_rows(hat, 8), own_rows(grad, 9)
+            scale = own_rows(jnp.broadcast_to(scale, (total, width)), 10)
+        else:
+            d_bias = transpose_rows(d_bias, 5 + layer)
+        sums = [row_sums(scratch, start, rows_wanted) for scratch in (many, more)]
+        wide = 2 * heads_wide
+        d_hat = times_stacked_t(jnp.concatenate([sums[1], d_gate], axis=1), in_ref[layer][:, wide : 2 * wide])
+        d_hat = d_hat + times_stacked_t(jnp.concatenate([d_q, sums[0]], axis=1), in_ref[layer][:, :wide])
+        d_hat = d_hat + times_stacked_t(d_bias, in_ref[layer][:, 2 * wide :])
         inner = d_hat - jnp.mean(d_hat, axis=-1, keepdims=True)
         inner = inner - hat * jnp.mean(d_hat * hat, axis=-1, keepdims=True)
         return grad + inner * scale
 
     pair_two, saved_start = forward(0, pair_one)
-    turned, saved_end = forward(1, transpose_rows(pair_two, 0))
-    turns[3] = turned
-    out_ref[0] = turns[3, pl.ds(me, n, stride=n), :]
-    grad = backward(1, transpose_rows(cot, 1), saved_end)
-    grad = backward(0, transpose_rows(grad, 2), saved_start)
-    turns[4] = grad
-    grad_ref[0] = turns[4, pl.ds(pl.multiple_of(me * n, SUBLANES), n), :]
+    turned_two = transpose_rows(pair_two, 0)
+    own_two = turns[0, pl.ds(pl.multiple_of(me * n, SUBLANES), n), :]
+    out_ref[0], saved_end = forward(1, turned_two, own_two)
+    grad = backward(1, transpose_rows(cot, 1), saved_end, False)
+    grad_ref[0] = backward(0, transpose_rows(grad, 2), saved_start, True)
 
 
 def spec(space=pltpu.VMEM):
@@ -478,7 +501,7 @@
     swap = opposite(2, 1)
     square = n * n
     bias = jnp.swapaxes(tri_bias, 1, 2)
-    firsts = (alignment, align_mask.T, align_gain[None], outer_in.T, pair_acts, pair_cotangent)
+    firsts = (alignment, outer_in.T, align_gain[None], align_mask.T, pair_acts, pair_cotangent)
     payload = pl.pallas_call(
         project_kernel,
         out_shape=jax.ShapeDtypeStruct((seqs // 2 + n + SUBLANES, LANES), F32),
@@ -534,7 +557,7 @@
             pltpu.VMEM((layers, square, inner), F32),
             pltpu.VMEM((layers, square, inner), F32),
             pltpu.VMEM((layers, square, inner), F32),
-            pltpu.VMEM((5 + layers, square, width), F32),
+            pltpu.VMEM((9 + layers, square, width), F32),
             pltpu.VMEM((square * n, inner), F32),
             pltpu.VMEM((square * n, inner), F32),
         ],

time: 22.8 us -> 22.5 us (0.987)
  Pallas kernels: 7.67 us -> 7.43 us
  transfers between devices with their start and end apart: 7 -> 7, of which waited for: 3 -> 3; matrix products, arithmetic and copies ran while one was open for 0% -> 0% of each run, Pallas kernels for 8% -> 9%
where the time goes in v3:
time: 22.5 us; the launch traced here: 22.3 us
  starting transfers between devices  8.64 us (38%)
  Pallas kernels  7.43 us (33%)
  waiting for transfers between devices  4.41 us (20%)
  local copies, waits for them, and re-layouts  1.06 us (5%)
  between operations  0.73 us (3%)
    ppermute x3, starting transfers between devices, gathered(): got = lax.ppermute(held, ('row', 'head', 'br'), pairs)  7.16 us
    ppermute x3, waiting for transfers between devices, gathered(): got = lax.ppermute(held, ('row', 'head', 'br'), pairs)  4.4 us
    pallas_call x1, Pallas kernels, gathered(): pl.pallas_call(functools.partial(part_kernel, 2 * heads), out_shape=(shap...  4.2 us
    pallas_call x1, Pallas kernels, gathered(): pl.pallas_call(project_kernel, out_shape=jax.ShapeDtypeStruct((seqs // 2...  1.32 us
    pallas_call x2, Pallas kernels, gathered(): pl.pallas_call(functools.partial(weights_kernel, layer), out_shape=(jax.S...  1.07 us
    unnamed x12, local copies, waits for them, and re-layouts  1.06 us
    ppermute x3, starting transfers between devices, gathered(): peers.append(lax.ppermute(value, 'br', swap))  0.91 us
    pallas_call x1, Pallas kernels, gathered(): pl.pallas_call(table_kernel, out_shape=(jax.ShapeDtypeStruct((outer_out.s...  0.84 us
  transfers between devices with their start and end apart: 7, of which 3 were waited for; matrix products, arithmetic and copies ran while one was open for 0% of the time, Pallas kernels for 9%

profile of v3, /device:TPU:0, one launch (start us, length us, event | category | flops | bytes accessed | tf_op | source)
XLA Modules:
  0.0 22.3 jit_solution(1679815790280737694)
XLA Ops:
  0.6 1.3 %project.1 = f32[24,128]{1,0:T(8,128)S(1)} custom-call(f32[16,1,256]{2,1,0:T(1,128)} %refs_0_.1, f32[64,256]{1,0:T(8,128)} %bitcast.12, f32[1,256]{1,0:T(1,128)} %bitcast.13, s32[1,32]{1,0:T(1,128)} %bitcast.14, f32[1,8,128]{2,1,0:T(8,128)} %refs_4_.1, f32[1,8,128]{2,1,0:T(8,128)} %refs_5_.1), custom_call_target="tpu_custom_call" | custom-call | tf_op jit(solution)/shard_map/project/pallas_call | solution.py:505
  2.0 3.6 %collective-permute-start = (f32[1,24,128]{2,1,0:T(8,128)S(1)}, f32[1,24,128]{2,1,0:T(8,128)S(1)}, u32[]{:S(2)}, u32[]{:S(2)}) collective-permute-start(f32[1,24,128]{2,1,0:T(8,128)S(1)} %bitcast.5), channel_id=1, source_target_pairs={{0,9},{1,8},{2,11},{3,10},{4,13},{5,12},{6,15},{7,14},{8,1},{9,0},... | collective-permute-start | bytes 36872 | tf_op jit(solution)/shard_map/ppermute | solution.py:546
  5.5 1.4 %collective-permute-done = f32[1,24,128]{2,1,0:T(8,128)S(1)} collective-permute-done((f32[1,24,128]{2,1,0:T(8,128)S(1)}, f32[1,24,128]{2,1,0:T(8,128)S(1)}, u32[]{:S(2)}, u32[]{:S(2)}) %collective-permute-start) | collective-permute-done | bytes 12320 | tf_op jit(solution)/shard_map/ppermute | solution.py:546
  6.9 1.9 %collective-permute-start.1 = (f32[2,24,128]{2,1,0:T(8,128)S(1)}, f32[2,24,128]{2,1,0:T(8,128)S(1)}, u32[]{:S(2)}, u32[]{:S(2)}) collective-permute-start(f32[2,24,128]{2,1,0:T(8,128)S(1)} %pad_maximum_fusion.2), channel_id=1, source_target_pairs={{0,5},{1,4},{2,7},{3,6},{4,1},{5,0},{6,3},{7,2},{8,13},{9,12},{10,... | collective-permute-start | bytes 73736 | tf_op jit(solution)/shard_map/ppermute | solution.py:546
  8.8 0.4 %collective-permute-start.4 = (f32[2,128,2,128]{3,2,1,0:T(2,128)}, f32[2,128,2,128]{3,2,1,0:T(2,128)S(1)}, u32[]{:S(2)}, u32[]{:S(2)}) collective-permute-start(f32[2,128,2,128]{3,2,1,0:T(2,128)} %own_in.3), channel_id=1, source_target_pairs={{0,1},{1,0},{2,3},{3,2},{4,5},{5,4},{6,7},{7,6},{8,9},{9,8},{10,11... | collective-permute-start | bytes 786440 | tf_op jit(solution)/shard_map/ppermute | solution.py:529
  9.2 1.1 %collective-permute-done.1 = f32[2,24,128]{2,1,0:T(8,128)S(1)} collective-permute-done((f32[2,24,128]{2,1,0:T(8,128)S(1)}, f32[2,24,128]{2,1,0:T(8,128)S(1)}, u32[]{:S(2)}, u32[]{:S(2)}) %collective-permute-start.1) | collective-permute-done | bytes 24608 | tf_op jit(solution)/shard_map/ppermute | solution.py:546
  10.3 0.0 copy-start.2
  10.4 0.0 copy-start.3
  10.4 1.7 %collective-permute-start.2 = (f32[4,24,128]{2,1,0:T(8,128)S(1)}, f32[4,24,128]{2,1,0:T(8,128)S(1)}, u32[]{:S(2)}, u32[]{:S(2)}) collective-permute-start(f32[4,24,128]{2,1,0:T(8,128)S(1)} %pad_maximum_fusion.1), channel_id=1, source_target_pairs={{0,3},{1,2},{2,1},{3,0},{4,7},{5,6},{6,5},{7,4},{8,11},{9,10},{10,... | collective-permute-start | bytes 147464 | tf_op jit(solution)/shard_map/ppermute | solution.py:546
  12.1 1.9 %collective-permute-done.2 = f32[4,24,128]{2,1,0:T(8,128)S(1)} collective-permute-done((f32[4,24,128]{2,1,0:T(8,128)S(1)}, f32[4,24,128]{2,1,0:T(8,128)S(1)}, u32[]{:S(2)}, u32[]{:S(2)}) %collective-permute-start.2) | collective-permute-done | bytes 49184 | tf_op jit(solution)/shard_map/ppermute | solution.py:546
  13.9 0.0 copy-start.5
  14.0 0.6 %collective-permute-start.3 = (f32[8,24,128]{2,1,0:T(8,128)S(1)}, f32[8,24,128]{2,1,0:T(8,128)S(1)}, u32[]{:S(2)}, u32[]{:S(2)}) collective-permute-start(f32[8,24,128]{2,1,0:T(8,128)S(1)} %pad_maximum_fusion.own_ref), channel_id=1, source_target_pairs={{0,1},{1,0},{2,3},{3,2},{4,5},{5,4},{6,7},{7,6},{8,9},{9,8},{10,11... | collective-permute-start | bytes 294920 | tf_op jit(solution)/shard_map/ppermute | solution.py:548
  14.5 0.0 copy-done.2
  14.5 0.1 collective-permute-start.6
  14.6 0.0 copy-done.3
  14.6 0.0 copy-start
  14.6 0.4 %collective-permute-start.5 = (f32[2,2,128]{2,1,0:T(2,128)S(1)}, f32[2,2,128]{2,1,0:T(2,128)S(1)}, u32[]{:S(2)}, u32[]{:S(2)}) collective-permute-start(f32[2,2,128]{2,1,0:T(2,128)S(1)} %bitcast.9), channel_id=1, source_target_pairs={{0,1},{1,0},{2,3},{3,2},{4,5},{5,4},{6,7},{7,6},{8,9},{9,8},{10,11... | collective-permute-start | bytes 6152 | tf_op jit(solution)/shard_map/ppermute | solution.py:529
  15.0 0.0 copy-done.5
  15.1 0.0 copy-start.1
  15.1 1.0 %copy-done.1 = f32[1024,128]{1,0:T(8,128)S(1)} copy-done((f32[1024,128]{1,0:T(8,128)S(1)}, f32[1024,128]{1,0:T(8,128)}, u32[]{:S(2)}) %copy-start.1) | copy-done | bytes 524312
  16.1 0.0 copy-start.4
  16.1 0.8 %table.1 = (bf16[1024,256]{1,0:T(8,128)(2,1)S(1)}, f32[8,128]{1,0:T(8,128)S(1)}) custom-call(f32[1024,128]{1,0:T(8,128)S(1)} %copy-done.1, s32[8]{0:T(128)S(1)} %copy-done.5), custom_call_target="tpu_custom_call" | custom-call | flops 4194304 | bytes 1048576 | tf_op jit(solution)/shard_map/table/pallas_call | solution.py:515
  16.9 0.0 collective-permute-done.5.peer_bias
  16.9 0.0 collective-permute-done.6.peer_out
  17.0 0.0 collective-permute-done.4.peer_in
  17.0 0.0 copy-done
  17.0 0.0 copy-done.4
  17.0 0.5 %shard_map.132 = (bf16[256,640]{1,0:T(8,128)(2,1)S(1)}, bf16[256,128]{1,0:T(8,128)(2,1)S(1)}) custom-call(f32[2,128]{1,0:T(2,128)S(1)} %copy-done.4, f32[2,128,2,128]{3,2,1,0:T(2,128)S(1)} %copy-done, f32[2,128,2,128]{3,2,1,0:T(2,128)S(1)} %collective-permute-done.4.peer_in, f32[2,2,128]{2,1,0:T(2,128)S(1)} %bitcast.10, ...), custom_call_target="tpu_custom_call" | custom-call | flops 4194304 | bytes 1048576 | tf_op jit(solution)/shard_map/pallas_call | solution.py:532
  17.5 0.5 %shard_map.131 = (bf16[256,640]{1,0:T(8,128)(2,1)S(1)}, bf16[256,128]{1,0:T(8,128)(2,1)S(1)}) custom-call(f32[2,128]{1,0:T(2,128)S(1)} %copy-done.4, f32[2,128,2,128]{3,2,1,0:T(2,128)S(1)} %copy-done, f32[2,128,2,128]{3,2,1,0:T(2,128)S(1)} %collective-permute-done.4.peer_in, f32[2,2,128]{2,1,0:T(2,128)S(1)} %bitcast.11, ...), custom_call_target="tpu_custom_call" | custom-call | flops 4194304 | bytes 1048576 | tf_op jit(solution)/shard_map/pallas_call | solution.py:532
  18.1 0.0 collective-permute-done.3.peer_ref
  18.1 4.2 %part.1 = (f32[1,8,128]{2,1,0:T(8,128)}, f32[1,8,128]{2,1,0:T(8,128)}) custom-call(f32[8,24,128]{2,1,0:T(8,128)S(1)} %pad_maximum_fusion.own_ref, f32[8,24,128]{2,1,0:T(8,128)S(1)} %collective-permute-done.3.peer_ref, f32[8,128]{1,0:T(8,128)S(1)} %get-tuple-element.8.live_ref, bf16[256,640]{1,0:T(8,128)(2,1)S(1)} %get-tuple-element.9.in_0, ...), custom_call_target="tpu_custom_call" | custom-call | tf_op jit(solution)/shard_map/part/pallas_call | solution.py:550
  (3 shorter events, 0.0 us)
Async XLA Ops:
  2.0 5.0 %collective-permute-start = (f32[1,24,128]{2,1,0:T(8,128)S(1)}, f32[1,24,128]{2,1,0:T(8,128)S(1)}, u32[]{:S(2)}, u32[]{:S(2)}) collective-permute-start(f32[1,24,128]{2,1,0:T(8,128)S(1)} %bitcast.5), channel_id=1, source_target_pairs={{0,9},{1,8},{2,11},{3,10},{4,13},{5,12},{6,15},{7,14},{8,1},{9,0},... | collective-permute-start | bytes 36872 | tf_op jit(solution)/shard_map/ppermute | solution.py:546
  6.9 3.4 %collective-permute-start.1 = (f32[2,24,128]{2,1,0:T(8,128)S(1)}, f32[2,24,128]{2,1,0:T(8,128)S(1)}, u32[]{:S(2)}, u32[]{:S(2)}) collective-permute-start(f32[2,24,128]{2,1,0:T(8,128)S(1)} %pad_maximum_fusion.2), channel_id=1, source_target_pairs={{0,5},{1,4},{2,7},{3,6},{4,1},{5,0},{6,3},{7,2},{8,13},{9,12},{10,... | collective-permute-start | bytes 73736 | tf_op jit(solution)/shard_map/ppermute | solution.py:546
  8.8 8.1 %collective-permute-start.4 = (f32[2,128,2,128]{3,2,1,0:T(2,128)}, f32[2,128,2,128]{3,2,1,0:T(2,128)S(1)}, u32[]{:S(2)}, u32[]{:S(2)}) collective-permute-start(f32[2,128,2,128]{3,2,1,0:T(2,128)} %own_in.3), channel_id=1, source_target_pairs={{0,1},{1,0},{2,3},{3,2},{4,5},{5,4},{6,7},{7,6},{8,9},{9,8},{10,11... | collective-permute-start | bytes 786440 | tf_op jit(solution)/shard_map/ppermute | solution.py:529
  10.3 4.2 %copy-start.2 = (f32[2,2,32,128]{3,2,1,0:T(8,128)S(1)}, f32[2,2,32,128]{3,2,1,0:T(8,128)}, u32[]{:S(2)}) copy-start(f32[2,2,32,128]{3,2,1,0:T(8,128)} %own_out.3) | copy-start | bytes 196612
  10.4 4.3 %copy-start.3 = (f32[2,128,2]{1,2,0:T(2,128)S(1)}, f32[2,128,2]{1,2,0:T(2,128)}, u32[]{:S(2)}) copy-start(f32[2,128,2]{1,2,0:T(2,128)} %param.21) | copy-start | bytes 6148
  10.4 3.6 %collective-permute-start.2 = (f32[4,24,128]{2,1,0:T(8,128)S(1)}, f32[4,24,128]{2,1,0:T(8,128)S(1)}, u32[]{:S(2)}, u32[]{:S(2)}) collective-permute-start(f32[4,24,128]{2,1,0:T(8,128)S(1)} %pad_maximum_fusion.1), channel_id=1, source_target_pairs={{0,3},{1,2},{2,1},{3,0},{4,7},{5,6},{6,5},{7,4},{8,11},{9,10},{10,... | collective-permute-start | bytes 147464 | tf_op jit(solution)/shard_map/ppermute | solution.py:546
  13.9 1.1 %copy-start.5 = (s32[8]{0:T(128)S(1)}, s32[8]{0:T(128)}, u32[]{:S(2)}) copy-start(s32[8]{0:T(128)} %live_ref.1) | copy-start | bytes 100
  14.0 4.1 %collective-permute-start.3 = (f32[8,24,128]{2,1,0:T(8,128)S(1)}, f32[8,24,128]{2,1,0:T(8,128)S(1)}, u32[]{:S(2)}, u32[]{:S(2)}) collective-permute-start(f32[8,24,128]{2,1,0:T(8,128)S(1)} %pad_maximum_fusion.own_ref), channel_id=1, source_target_pairs={{0,1},{1,0},{2,3},{3,2},{4,5},{5,4},{6,7},{7,6},{8,9},{9,8},{10,11... | collective-permute-start | bytes 294920 | tf_op jit(solution)/shard_map/ppermute | solution.py:548
  14.5 2.4 %collective-permute-start.6 = (f32[2,2,32,128]{3,2,1,0:T(8,128)S(1)}, f32[2,2,32,128]{3,2,1,0:T(8,128)S(1)}, u32[]{:S(2)}, u32[]{:S(2)}) collective-permute-start(f32[2,2,32,128]{3,2,1,0:T(8,128)S(1)} %copy-done.2), channel_id=1, source_target_pairs={{0,1},{1,0},{2,3},{3,2},{4,5},{5,4},{6,7},{7,6},{8,9},{9,8},{10,11... | collective-permute-start | bytes 196616 | tf_op jit(solution)/shard_map/ppermute | solution.py:529
  14.6 2.4 %copy-start = (f32[2,128,2,128]{3,2,1,0:T(2,128)S(1)}, f32[2,128,2,128]{3,2,1,0:T(2,128)}, u32[]{:S(2)}) copy-start(f32[2,128,2,128]{3,2,1,0:T(2,128)} %own_in.3) | copy-start | bytes 786436
  14.6 2.3 %collective-permute-start.5 = (f32[2,2,128]{2,1,0:T(2,128)S(1)}, f32[2,2,128]{2,1,0:T(2,128)S(1)}, u32[]{:S(2)}, u32[]{:S(2)}) collective-permute-start(f32[2,2,128]{2,1,0:T(2,128)S(1)} %bitcast.9), channel_id=1, source_target_pairs={{0,1},{1,0},{2,3},{3,2},{4,5},{5,4},{6,7},{7,6},{8,9},{9,8},{10,11... | collective-permute-start | bytes 6152 | tf_op jit(solution)/shard_map/ppermute | solution.py:529
  15.1 1.0 %copy-start.1 = (f32[1024,128]{1,0:T(8,128)S(1)}, f32[1024,128]{1,0:T(8,128)}, u32[]{:S(2)}) copy-start(f32[1024,128]{1,0:T(8,128)} %table_ref.1) | copy-start | bytes 1572868
  16.1 0.9 %copy-start.4 = (f32[2,128]{1,0:T(2,128)S(1)}, f32[2,128]{1,0:T(2,128)}, u32[]{:S(2)}) copy-start(f32[2,128]{1,0:T(2,128)} %gain_ref.3) | copy-start | bytes 3076

commit v4 on v3

--- a/solution.py
+++ b/solution.py
@@ -176,7 +176,7 @@
     average = jnp.mean(values, axis=-1, keepdims=True)
     centred = values - average
     scale = lax.rsqrt(jnp.mean(centred * centred, axis=-1, keepdims=True) + EPSILON)
-    return centred * scale, scale
+    return centred, scale
 
 
 def regroup(blocks, width):
@@ -201,7 +201,8 @@
     seqs, _, width = align_ref.shape
     rows = seqs // 2
     copies[0].wait()
-    normed, _ = centre(jnp.reshape(align_ref[...], (seqs, width)))
+    centred, scale = centre(jnp.reshape(align_ref[...], (seqs, width)))
+    normed = centred * scale
     copies[1].wait()
     stacked = jnp.concatenate(split2(proj_ref[...]), axis=0)
     copies[2].wait()
@@ -222,11 +223,11 @@
     out_ref[0:rows, :] = jnp.concatenate([projected[:rows], projected[rows:]], axis=1)
 
 
-def weights_kernel(layer, gain_ref, own_in, peer_in, own_bias, peer_bias, own_out, peer_out, in_ref, out_ref):
+def weights_kernel(layer, gain_ref, own_in, peer_in, own_bias, peer_bias, own_out, peer_out, in_ref, out_ref, *both_ref):
     first = lax.axis_index("br") == 0
     heads, width = own_in.shape[2:]
     size = width // 4
-    blocks, lines, ends = [], [], []
+    blocks, lines, ends, before = [], [], [], []
     for half in range(2):
         pick = first if half == 0 else jnp.logical_not(first)
         for h in range(heads):
@@ -234,11 +235,18 @@
             bias = jnp.where(pick, own_bias[layer, h : h + 1, :], peer_bias[layer, h : h + 1, :])
             lines.append(jnp.broadcast_to(bias, (size, bias.shape[1])))
             ends.append(jnp.where(pick, own_out[layer, h], peer_out[layer, h]))
+            if both_ref:
+                before.append(jnp.where(pick, own_out[layer - 1, h], peer_out[layer - 1, h]))
     table = jnp.concatenate(regroup(blocks, size) + [jnp.concatenate(lines, axis=0).T], axis=1)
     gain = gain_ref[layer : layer + 1, :]
     table = table * jnp.broadcast_to(gain, (gain.shape[1], gain.shape[1])).T[:, :1]
     in_ref[...] = jnp.concatenate(split2(table), axis=0)
     out_ref[...] = jnp.concatenate(split2(jnp.concatenate(ends, axis=0)), axis=0)
+    if both_ref:
+        before = jnp.concatenate(before, axis=0)
+        before = before - jnp.mean(before, axis=-1, keepdims=True)
+        both = times_stacked(before, in_ref[...])
+        both_ref[0][...] = jnp.concatenate(split2(both), axis=0)
 
 
 def table_kernel(table_ref, live_ref, out_ref, rows_ref):
@@ -253,7 +261,7 @@
 
 
 def part_kernel(
-    heads, own_ref, peer_ref, live_ref, in_0, end_0, in_1, end_1, table_ref, out_ref, grad_ref,
+    heads, own_ref, peer_ref, live_ref, in_0, end_0, in_1, end_1, both_ref, table_ref, out_ref, grad_ref,
     mixed, keys, vals, lines, turns, many, more,
 ):
     me = lax.axis_index(("row", "head"))
@@ -330,12 +338,22 @@
     def block(values, i):
         return values[i * n : (i + 1) * n]
 
-    def forward(layer, entry, own_entry=None):
-        hat, scale = centre(entry)
+    def forward(layer, entry, own_entry=None, lead=None):
+        centred, scale = centre(entry)
+        hat = centred * scale
+
+        def project(start, stop):
+            weights = in_ref[layer][:, start:stop]
+            if lead is None:
+                return times_stacked(hat, weights)
+            entered, added = lead
+            whole = times_stacked(entered, weights) + times_stacked(added, both_ref[:, start:stop])
+            return whole * scale
+
         wide = 2 * heads_wide
-        pair_qk = times_stacked(hat, in_ref[layer][:, :wide])
-        pair_vg = times_stacked(hat, in_ref[layer][:, wide : 2 * wide])
-        bias = times_stacked(hat, in_ref[layer][:, 2 * wide :])
+        pair_qk = project(0, wide)
+        pair_vg = project(wide, 2 * wide)
+        bias = project(2 * wide, in_ref[layer].shape[1])
         q, k = pair_qk[:, :heads_wide], pair_qk[:, heads_wide:]
         v, gate = pair_vg[:, :heads_wide], pair_vg[:, heads_wide:]
         q = q * factor
@@ -367,13 +385,15 @@
             attended.append(mix)
         attended = jnp.concatenate(attended, axis=0)
         opened = jax.nn.sigmoid(gate)
-        gated, mask = opened * attended, pair_mask
+        gated = opened * attended
         if own_entry is not None:
             turns[3] = gated
             gated, entry = turns[3, pl.ds(me, n, stride=n), :], own_entry
-            mask = live * live_ref[pl.ds(me, 1), :]
-        update = times_stacked(gated, end_ref[layer][...])
-        return entry + update * mask, (hat, scale, q, opened, attended, probs)
+            gated = gated * (live * live_ref[pl.ds(me, 1), :])
+        else:
+            gated = gated * pair_mask
+        left = (hat, scale, q, opened, attended, probs)
+        return entry + times_stacked(gated, end_ref[layer][...]), left, (centred, gated)
 
     def row_sums(scratch, start, size):
         whole = scratch[pl.ds(start, size, stride=n), :]
@@ -434,10 +454,11 @@
         inner = inner - hat * jnp.mean(d_hat * hat, axis=-1, keepdims=True)
         return grad + inner * scale
 
-    pair_two, saved_start = forward(0, pair_one)
+    pair_two, saved_start, (entered, added) = forward(0, pair_one)
     turned_two = transpose_rows(pair_two, 0)
     own_two = turns[0, pl.ds(pl.multiple_of(me * n, SUBLANES), n), :]
-    out_ref[0], saved_end = forward(1, turned_two, own_two)
+    lead = (transpose_rows(entered, 11), transpose_rows(added, 12))
+    out_ref[0], saved_end, _ = forward(1, turned_two, own_two, lead)
     grad = backward(1, transpose_rows(cot, 1), saved_end, False)
     grad_ref[0] = backward(0, transpose_rows(grad, 2), saved_start, True)
 
@@ -534,9 +555,10 @@
             out_shape=(
                 jax.ShapeDtypeStruct((2 * width, 5 * inner), BF16),
                 jax.ShapeDtypeStruct((2 * inner, width), BF16),
-            ),
+            )
+            + (jax.ShapeDtypeStruct((2 * inner, 5 * inner), BF16),) * min(layer, 1),
             in_specs=[spec()] * 7,
-            out_specs=(spec(), spec()),
+            out_specs=(spec(),) * (2 + min(layer, 1)),
             compiler_params=limit(4),
             cost_estimate=cost(1 << 22),
         )(tri_gain, tri_in, peers[0], bias, peers[1], tri_out, peers[2])
@@ -550,14 +572,14 @@
     return pl.pallas_call(
         functools.partial(part_kernel, 2 * heads),
         out_shape=(shape, shape),
-        in_specs=[spec()] * 8,
+        in_specs=[spec()] * 9,
         out_specs=(spec(), spec()),
         scratch_shapes=[
             pltpu.VMEM((n * OPC // LANES, n * OPC, LANES), F32),
             pltpu.VMEM((layers, square, inner), F32),
             pltpu.VMEM((layers, square, inner), F32),
             pltpu.VMEM((layers, square, inner), F32),
-            pltpu.VMEM((9 + layers, square, width), F32),
+            pltpu.VMEM((11 + layers, square, width), F32),
             pltpu.VMEM((square * n, inner), F32),
             pltpu.VMEM((square * n, inner), F32),
         ],

time: 22.5 us -> 22.6 us (level)
  no operation moved by 1% of the time
where the time goes in v4:
time: 22.6 us; the launch traced here: 22.4 us
  starting transfers between devices  8.64 us (38%)
  Pallas kernels  7.52 us (33%)
  waiting for transfers between devices  4.41 us (20%)
  local copies, waits for them, and re-layouts  1.06 us (5%)
  between operations  0.73 us (3%)
    ppermute x3, starting transfers between devices, gathered(): got = lax.ppermute(held, ('row', 'head', 'br'), pairs)  7.16 us
    ppermute x3, waiting for transfers between devices, gathered(): got = lax.ppermute(held, ('row', 'head', 'br'), pairs)  4.4 us
    pallas_call x1, Pallas kernels, gathered(): pl.pallas_call(functools.partial(part_kernel, 2 * heads), out_shape=(shap...  4.11 us
    pallas_call x1, Pallas kernels, gathered(): pl.pallas_call(project_kernel, out_shape=jax.ShapeDtypeStruct((seqs // 2...  1.32 us
    pallas_call x2, Pallas kernels, gathered(): pl.pallas_call(functools.partial(weights_kernel, layer), out_shape=(jax.S...  1.24 us
    unnamed x12, local copies, waits for them, and re-layouts  1.06 us
    ppermute x3, starting transfers between devices, gathered(): peers.append(lax.ppermute(value, 'br', swap))  0.91 us
    pallas_call x1, Pallas kernels, gathered(): pl.pallas_call(table_kernel, out_shape=(jax.ShapeDtypeStruct((outer_out.s...  0.84 us
  transfers between devices with their start and end apart: 7, of which 3 were waited for; matrix products, arithmetic and copies ran while one was open for 0% of the time, Pallas kernels for 9%

profile of v4, /device:TPU:0, one launch (start us, length us, event | category | flops | bytes accessed | tf_op | source)
XLA Modules:
  0.0 22.4 jit_solution(17261548352637794403)
XLA Ops:
  0.6 1.3 %project.1 = f32[24,128]{1,0:T(8,128)S(1)} custom-call(f32[16,1,256]{2,1,0:T(1,128)} %refs_0_.1, f32[64,256]{1,0:T(8,128)} %bitcast.12, f32[1,256]{1,0:T(1,128)} %bitcast.13, s32[1,32]{1,0:T(1,128)} %bitcast.14, f32[1,8,128]{2,1,0:T(8,128)} %refs_4_.1, f32[1,8,128]{2,1,0:T(8,128)} %refs_5_.1), custom_call_target="tpu_custom_call" | custom-call | tf_op jit(solution)/shard_map/project/pallas_call | solution.py:526
  2.0 3.6 %collective-permute-start = (f32[1,24,128]{2,1,0:T(8,128)S(1)}, f32[1,24,128]{2,1,0:T(8,128)S(1)}, u32[]{:S(2)}, u32[]{:S(2)}) collective-permute-start(f32[1,24,128]{2,1,0:T(8,128)S(1)} %bitcast.5), channel_id=1, source_target_pairs={{0,9},{1,8},{2,11},{3,10},{4,13},{5,12},{6,15},{7,14},{8,1},{9,0},... | collective-permute-start | bytes 36872 | tf_op jit(solution)/shard_map/ppermute | solution.py:568
  5.5 1.4 %collective-permute-done = f32[1,24,128]{2,1,0:T(8,128)S(1)} collective-permute-done((f32[1,24,128]{2,1,0:T(8,128)S(1)}, f32[1,24,128]{2,1,0:T(8,128)S(1)}, u32[]{:S(2)}, u32[]{:S(2)}) %collective-permute-start) | collective-permute-done | bytes 12320 | tf_op jit(solution)/shard_map/ppermute | solution.py:568
  6.9 1.9 %collective-permute-start.1 = (f32[2,24,128]{2,1,0:T(8,128)S(1)}, f32[2,24,128]{2,1,0:T(8,128)S(1)}, u32[]{:S(2)}, u32[]{:S(2)}) collective-permute-start(f32[2,24,128]{2,1,0:T(8,128)S(1)} %pad_maximum_fusion.2), channel_id=1, source_target_pairs={{0,5},{1,4},{2,7},{3,6},{4,1},{5,0},{6,3},{7,2},{8,13},{9,12},{10,... | collective-permute-start | bytes 73736 | tf_op jit(solution)/shard_map/ppermute | solution.py:568
  8.8 0.4 %collective-permute-start.4 = (f32[2,128,2,128]{3,2,1,0:T(2,128)}, f32[2,128,2,128]{3,2,1,0:T(2,128)S(1)}, u32[]{:S(2)}, u32[]{:S(2)}) collective-permute-start(f32[2,128,2,128]{3,2,1,0:T(2,128)} %own_in.3), channel_id=1, source_target_pairs={{0,1},{1,0},{2,3},{3,2},{4,5},{5,4},{6,7},{7,6},{8,9},{9,8},{10,11... | collective-permute-start | bytes 786440 | tf_op jit(solution)/shard_map/ppermute | solution.py:550
  9.2 1.1 %collective-permute-done.1 = f32[2,24,128]{2,1,0:T(8,128)S(1)} collective-permute-done((f32[2,24,128]{2,1,0:T(8,128)S(1)}, f32[2,24,128]{2,1,0:T(8,128)S(1)}, u32[]{:S(2)}, u32[]{:S(2)}) %collective-permute-start.1) | collective-permute-done | bytes 24608 | tf_op jit(solution)/shard_map/ppermute | solution.py:568
  10.3 0.0 copy-start.2
  10.4 0.0 copy-start.3
  10.4 1.7 %collective-permute-start.2 = (f32[4,24,128]{2,1,0:T(8,128)S(1)}, f32[4,24,128]{2,1,0:T(8,128)S(1)}, u32[]{:S(2)}, u32[]{:S(2)}) collective-permute-start(f32[4,24,128]{2,1,0:T(8,128)S(1)} %pad_maximum_fusion.1), channel_id=1, source_target_pairs={{0,3},{1,2},{2,1},{3,0},{4,7},{5,6},{6,5},{7,4},{8,11},{9,10},{10,... | collective-permute-start | bytes 147464 | tf_op jit(solution)/shard_map/ppermute | solution.py:568
  12.1 1.9 %collective-permute-done.2 = f32[4,24,128]{2,1,0:T(8,128)S(1)} collective-permute-done((f32[4,24,128]{2,1,0:T(8,128)S(1)}, f32[4,24,128]{2,1,0:T(8,128)S(1)}, u32[]{:S(2)}, u32[]{:S(2)}) %collective-permute-start.2) | collective-permute-done | bytes 49184 | tf_op jit(solution)/shard_map/ppermute | solution.py:568
  13.9 0.0 copy-start.5
  14.0 0.6 %collective-permute-start.3 = (f32[8,24,128]{2,1,0:T(8,128)S(1)}, f32[8,24,128]{2,1,0:T(8,128)S(1)}, u32[]{:S(2)}, u32[]{:S(2)}) collective-permute-start(f32[8,24,128]{2,1,0:T(8,128)S(1)} %pad_maximum_fusion.own_ref), channel_id=1, source_target_pairs={{0,1},{1,0},{2,3},{3,2},{4,5},{5,4},{6,7},{7,6},{8,9},{9,8},{10,11... | collective-permute-start | bytes 294920 | tf_op jit(solution)/shard_map/ppermute | solution.py:570
  14.5 0.0 copy-done.2
  14.5 0.1 collective-permute-start.6
  14.6 0.0 copy-done.3
  14.6 0.0 copy-start
  14.6 0.4 %collective-permute-start.5 = (f32[2,2,128]{2,1,0:T(2,128)S(1)}, f32[2,2,128]{2,1,0:T(2,128)S(1)}, u32[]{:S(2)}, u32[]{:S(2)}) collective-permute-start(f32[2,2,128]{2,1,0:T(2,128)S(1)} %bitcast.9), channel_id=1, source_target_pairs={{0,1},{1,0},{2,3},{3,2},{4,5},{5,4},{6,7},{7,6},{8,9},{9,8},{10,11... | collective-permute-start | bytes 6152 | tf_op jit(solution)/shard_map/ppermute | solution.py:550
  15.0 0.0 copy-done.5
  15.1 0.0 copy-start.1
  15.1 1.0 %copy-done.1 = f32[1024,128]{1,0:T(8,128)S(1)} copy-done((f32[1024,128]{1,0:T(8,128)S(1)}, f32[1024,128]{1,0:T(8,128)}, u32[]{:S(2)}) %copy-start.1) | copy-done | bytes 524312
  16.1 0.0 copy-start.4
  16.1 0.8 %table.1 = (bf16[1024,256]{1,0:T(8,128)(2,1)S(1)}, f32[8,128]{1,0:T(8,128)S(1)}) custom-call(f32[1024,128]{1,0:T(8,128)S(1)} %copy-done.1, s32[8]{0:T(128)S(1)} %copy-done.5), custom_call_target="tpu_custom_call" | custom-call | flops 4194304 | bytes 1048576 | tf_op jit(solution)/shard_map/table/pallas_call | solution.py:536
  16.9 0.0 collective-permute-done.5.peer_bias
  16.9 0.0 collective-permute-done.6.peer_out
  17.0 0.0 collective-permute-done.4.peer_in
  17.0 0.0 copy-done
  17.0 0.0 copy-done.4
  17.0 0.5 %shard_map.131 = (bf16[256,640]{1,0:T(8,128)(2,1)S(1)}, bf16[256,128]{1,0:T(8,128)(2,1)S(1)}) custom-call(f32[2,128]{1,0:T(2,128)S(1)} %copy-done.4, f32[2,128,2,128]{3,2,1,0:T(2,128)S(1)} %copy-done, f32[2,128,2,128]{3,2,1,0:T(2,128)S(1)} %collective-permute-done.4.peer_in, f32[2,2,128]{2,1,0:T(2,128)S(1)} %bitcast.10, ...), custom_call_target="tpu_custom_call" | custom-call | flops 4194304 | bytes 1048576 | tf_op jit(solution)/shard_map/pallas_call | solution.py:553
  17.5 0.7 %shard_map.132 = (bf16[256,640]{1,0:T(8,128)(2,1)S(1)}, bf16[256,128]{1,0:T(8,128)(2,1)S(1)}, bf16[256,640]{1,0:T(8,128)(2,1)S(1)}) custom-call(f32[2,128]{1,0:T(2,128)S(1)} %copy-done.4, f32[2,128,2,128]{3,2,1,0:T(2,128)S(1)} %copy-done, f32[2,128,2,128]{3,2,1,0:T(2,128)S(1)} %collective-permute-done.4.peer_in, f32[2,2,128]{2,1,0:T(2,128)S(1)} %bitcast.11, ...), custom_call_target="tpu_custom_call" | custom-call | flops 4194304 | bytes 1048576 | tf_op jit(solution)/shard_map/pallas_call | solution.py:553
  18.2 0.0 collective-permute-done.3.peer_ref
  18.3 4.1 %part.1 = (f32[1,8,128]{2,1,0:T(8,128)}, f32[1,8,128]{2,1,0:T(8,128)}) custom-call(f32[8,24,128]{2,1,0:T(8,128)S(1)} %pad_maximum_fusion.own_ref, f32[8,24,128]{2,1,0:T(8,128)S(1)} %collective-permute-done.3.peer_ref, f32[8,128]{1,0:T(8,128)S(1)} %get-tuple-element.9.live_ref, bf16[256,640]{1,0:T(8,128)(2,1)S(1)} %get-tuple-element.10.in_0, ...), custom_call_target="tpu_custom_call" | custom-call | tf_op jit(solution)/shard_map/part/pallas_call | solution.py:572
  (3 shorter events, 0.0 us)
Async XLA Ops:
  2.0 5.0 %collective-permute-start = (f32[1,24,128]{2,1,0:T(8,128)S(1)}, f32[1,24,128]{2,1,0:T(8,128)S(1)}, u32[]{:S(2)}, u32[]{:S(2)}) collective-permute-start(f32[1,24,128]{2,1,0:T(8,128)S(1)} %bitcast.5), channel_id=1, source_target_pairs={{0,9},{1,8},{2,11},{3,10},{4,13},{5,12},{6,15},{7,14},{8,1},{9,0},... | collective-permute-start | bytes 36872 | tf_op jit(solution)/shard_map/ppermute | solution.py:568
  6.9 3.4 %collective-permute-start.1 = (f32[2,24,128]{2,1,0:T(8,128)S(1)}, f32[2,24,128]{2,1,0:T(8,128)S(1)}, u32[]{:S(2)}, u32[]{:S(2)}) collective-permute-start(f32[2,24,128]{2,1,0:T(8,128)S(1)} %pad_maximum_fusion.2), channel_id=1, source_target_pairs={{0,5},{1,4},{2,7},{3,6},{4,1},{5,0},{6,3},{7,2},{8,13},{9,12},{10,... | collective-permute-start | bytes 73736 | tf_op jit(solution)/shard_map/ppermute | solution.py:568
  8.8 8.1 %collective-permute-start.4 = (f32[2,128,2,128]{3,2,1,0:T(2,128)}, f32[2,128,2,128]{3,2,1,0:T(2,128)S(1)}, u32[]{:S(2)}, u32[]{:S(2)}) collective-permute-start(f32[2,128,2,128]{3,2,1,0:T(2,128)} %own_in.3), channel_id=1, source_target_pairs={{0,1},{1,0},{2,3},{3,2},{4,5},{5,4},{6,7},{7,6},{8,9},{9,8},{10,11... | collective-permute-start | bytes 786440 | tf_op jit(solution)/shard_map/ppermute | solution.py:550
  10.3 4.2 %copy-start.2 = (f32[2,2,32,128]{3,2,1,0:T(8,128)S(1)}, f32[2,2,32,128]{3,2,1,0:T(8,128)}, u32[]{:S(2)}) copy-start(f32[2,2,32,128]{3,2,1,0:T(8,128)} %own_out.3) | copy-start | bytes 196612
  10.4 4.3 %copy-start.3 = (f32[2,128,2]{1,2,0:T(2,128)S(1)}, f32[2,128,2]{1,2,0:T(2,128)}, u32[]{:S(2)}) copy-start(f32[2,128,2]{1,2,0:T(2,128)} %param.21) | copy-start | bytes 6148
  10.4 3.6 %collective-permute-start.2 = (f32[4,24,128]{2,1,0:T(8,128)S(1)}, f32[4,24,128]{2,1,0:T(8,128)S(1)}, u32[]{:S(2)}, u32[]{:S(2)}) collective-permute-start(f32[4,24,128]{2,1,0:T(8,128)S(1)} %pad_maximum_fusion.1), channel_id=1, source_target_pairs={{0,3},{1,2},{2,1},{3,0},{4,7},{5,6},{6,5},{7,4},{8,11},{9,10},{10,... | collective-permute-start | bytes 147464 | tf_op jit(solution)/shard_map/ppermute | solution.py:568
  13.9 1.1 %copy-start.5 = (s32[8]{0:T(128)S(1)}, s32[8]{0:T(128)}, u32[]{:S(2)}) copy-start(s32[8]{0:T(128)} %live_ref.1) | copy-start | bytes 100
  14.0 4.3 %collective-permute-start.3 = (f32[8,24,128]{2,1,0:T(8,128)S(1)}, f32[8,24,128]{2,1,0:T(8,128)S(1)}, u32[]{:S(2)}, u32[]{:S(2)}) collective-permute-start(f32[8,24,128]{2,1,0:T(8,128)S(1)} %pad_maximum_fusion.own_ref), channel_id=1, source_target_pairs={{0,1},{1,0},{2,3},{3,2},{4,5},{5,4},{6,7},{7,6},{8,9},{9,8},{10,11... | collective-permute-start | bytes 294920 | tf_op jit(solution)/shard_map/ppermute | solution.py:570
  14.5 2.4 %collective-permute-start.6 = (f32[2,2,32,128]{3,2,1,0:T(8,128)S(1)}, f32[2,2,32,128]{3,2,1,0:T(8,128)S(1)}, u32[]{:S(2)}, u32[]{:S(2)}) collective-permute-start(f32[2,2,32,128]{3,2,1,0:T(8,128)S(1)} %copy-done.2), channel_id=1, source_target_pairs={{0,1},{1,0},{2,3},{3,2},{4,5},{5,4},{6,7},{7,6},{8,9},{9,8},{10,11... | collective-permute-start | bytes 196616 | tf_op jit(solution)/shard_map/ppermute | solution.py:550
  14.6 2.4 %copy-start = (f32[2,128,2,128]{3,2,1,0:T(2,128)S(1)}, f32[2,128,2,128]{3,2,1,0:T(2,128)}, u32[]{:S(2)}) copy-start(f32[2,128,2,128]{3,2,1,0:T(2,128)} %own_in.3) | copy-start | bytes 786436
  14.6 2.3 %collective-permute-start.5 = (f32[2,2,128]{2,1,0:T(2,128)S(1)}, f32[2,2,128]{2,1,0:T(2,128)S(1)}, u32[]{:S(2)}, u32[]{:S(2)}) collective-permute-start(f32[2,2,128]{2,1,0:T(2,128)S(1)} %bitcast.9), channel_id=1, source_target_pairs={{0,1},{1,0},{2,3},{3,2},{4,5},{5,4},{6,7},{7,6},{8,9},{9,8},{10,11... | collective-permute-start | bytes 6152 | tf_op jit(solution)/shard_map/ppermute | solution.py:550
  15.1 1.0 %copy-start.1 = (f32[1024,128]{1,0:T(8,128)S(1)}, f32[1024,128]{1,0:T(8,128)}, u32[]{:S(2)}) copy-start(f32[1024,128]{1,0:T(8,128)} %table_ref.1) | copy-start | bytes 1572868
  16.1 0.9 %copy-start.4 = (f32[2,128]{1,0:T(2,128)S(1)}, f32[2,128]{1,0:T(2,128)}, u32[]{:S(2)}) copy-start(f32[2,128]{1,0:T(2,128)} %gain_ref.3) | copy-start | bytes 3076

commit v5 on v4

--- a/solution.py
+++ b/solution.py
@@ -479,11 +479,15 @@
     return count.bit_length() - 1
 
 
+def step_bits(bits):
+    return [bits - 1, *range(bits - 1)]
+
+
 def reverse(index, bits):
-    back = 0
-    for k in range(bits):
-        back = back | (((index >> k) & 1) << (bits - 1 - k))
-    return back
+    slot = 0
+    for k, bit in enumerate(step_bits(bits)):
+        slot = slot | (((index >> bit) & 1) << k)
+    return slot
 
 
 def parity(index, bits):
@@ -563,8 +567,8 @@
             cost_estimate=cost(1 << 22),
         )(tri_gain, tri_in, peers[0], bias, peers[1], tri_out, peers[2])
     held = payload[None]
-    for at in range(bits_of(n)):
-        pairs = opposite(2 * n, (n >> at) | 1)
+    for bit in step_bits(bits_of(n)):
+        pairs = opposite(2 * n, (2 << bit) | 1)
         got = lax.ppermute(held, ("row", "head", "br"), pairs)
         held = jnp.concatenate([held, got], axis=0)
     other = lax.ppermute(held, "br", swap)

time: 22.6 us -> 22.6 us (level)
  no operation moved by 1% of the time
where the time goes in v5:
time: 22.6 us; the launch traced here: 22.4 us
  starting transfers between devices  8.67 us (38%)
  Pallas kernels  7.52 us (33%)
  waiting for transfers between devices  4.38 us (19%)
  local copies, waits for them, and re-layouts  1.06 us (5%)
  between operations  0.73 us (3%)
    ppermute x3, starting transfers between devices, gathered(): got = lax.ppermute(held, ('row', 'head', 'br'), pairs)  7.25 us
    ppermute x3, waiting for transfers between devices, gathered(): got = lax.ppermute(held, ('row', 'head', 'br'), pairs)  4.37 us
    pallas_call x1, Pallas kernels, gathered(): pl.pallas_call(functools.partial(part_kernel, 2 * heads), out_shape=(shap...  4.11 us
    pallas_call x1, Pallas kernels, gathered(): pl.pallas_call(project_kernel, out_shape=jax.ShapeDtypeStruct((seqs // 2...  1.32 us
    pallas_call x2, Pallas kernels, gathered(): pl.pallas_call(functools.partial(weights_kernel, layer), out_shape=(jax.S...  1.24 us
    unnamed x12, local copies, waits for them, and re-layouts  1.06 us
    ppermute x3, starting transfers between devices, gathered(): peers.append(lax.ppermute(value, 'br', swap))  0.91 us
    pallas_call x1, Pallas kernels, gathered(): pl.pallas_call(table_kernel, out_shape=(jax.ShapeDtypeStruct((outer_out.s...  0.84 us
  transfers between devices with their start and end apart: 7, of which 3 were waited for; matrix products, arithmetic and copies ran while one was open for 0% of the time, Pallas kernels for 9%

profile of v5, /device:TPU:0, one launch (start us, length us, event | category | flops | bytes accessed | tf_op | source)
XLA Modules:
  0.0 22.4 jit_solution(3425459516486357930)
XLA Ops:
  0.6 1.3 %project.1 = f32[24,128]{1,0:T(8,128)S(1)} custom-call(f32[16,1,256]{2,1,0:T(1,128)} %refs_0_.1, f32[64,256]{1,0:T(8,128)} %bitcast.12, f32[1,256]{1,0:T(1,128)} %bitcast.13, s32[1,32]{1,0:T(1,128)} %bitcast.14, f32[1,8,128]{2,1,0:T(8,128)} %refs_4_.1, f32[1,8,128]{2,1,0:T(8,128)} %refs_5_.1), custom_call_target="tpu_custom_call" | custom-call | tf_op jit(solution)/shard_map/project/pallas_call | solution.py:530
  2.0 3.6 %collective-permute-start = (f32[1,24,128]{2,1,0:T(8,128)S(1)}, f32[1,24,128]{2,1,0:T(8,128)S(1)}, u32[]{:S(2)}, u32[]{:S(2)}) collective-permute-start(f32[1,24,128]{2,1,0:T(8,128)S(1)} %bitcast.5), channel_id=1, source_target_pairs={{0,9},{1,8},{2,11},{3,10},{4,13},{5,12},{6,15},{7,14},{8,1},{9,0},... | collective-permute-start | bytes 36872 | tf_op jit(solution)/shard_map/ppermute | solution.py:572
  5.5 1.4 %collective-permute-done = f32[1,24,128]{2,1,0:T(8,128)S(1)} collective-permute-done((f32[1,24,128]{2,1,0:T(8,128)S(1)}, f32[1,24,128]{2,1,0:T(8,128)S(1)}, u32[]{:S(2)}, u32[]{:S(2)}) %collective-permute-start) | collective-permute-done | bytes 12320 | tf_op jit(solution)/shard_map/ppermute | solution.py:572
  6.9 1.8 %collective-permute-start.1 = (f32[2,24,128]{2,1,0:T(8,128)S(1)}, f32[2,24,128]{2,1,0:T(8,128)S(1)}, u32[]{:S(2)}, u32[]{:S(2)}) collective-permute-start(f32[2,24,128]{2,1,0:T(8,128)S(1)} %pad_maximum_fusion.2), channel_id=1, source_target_pairs={{0,3},{1,2},{2,1},{3,0},{4,7},{5,6},{6,5},{7,4},{8,11},{9,10},{10,... | collective-permute-start | bytes 73736 | tf_op jit(solution)/shard_map/ppermute | solution.py:572
  8.7 0.4 %collective-permute-start.4 = (f32[2,128,2,128]{3,2,1,0:T(2,128)}, f32[2,128,2,128]{3,2,1,0:T(2,128)S(1)}, u32[]{:S(2)}, u32[]{:S(2)}) collective-permute-start(f32[2,128,2,128]{3,2,1,0:T(2,128)} %own_in.3), channel_id=1, source_target_pairs={{0,1},{1,0},{2,3},{3,2},{4,5},{5,4},{6,7},{7,6},{8,9},{9,8},{10,11... | collective-permute-start | bytes 786440 | tf_op jit(solution)/shard_map/ppermute | solution.py:554
  9.1 1.1 %collective-permute-done.1 = f32[2,24,128]{2,1,0:T(8,128)S(1)} collective-permute-done((f32[2,24,128]{2,1,0:T(8,128)S(1)}, f32[2,24,128]{2,1,0:T(8,128)S(1)}, u32[]{:S(2)}, u32[]{:S(2)}) %collective-permute-start.1) | collective-permute-done | bytes 24608 | tf_op jit(solution)/shard_map/ppermute | solution.py:572
  10.3 0.0 copy-start.2
  10.3 0.0 copy-start.3
  10.3 1.9 %collective-permute-start.2 = (f32[4,24,128]{2,1,0:T(8,128)S(1)}, f32[4,24,128]{2,1,0:T(8,128)S(1)}, u32[]{:S(2)}, u32[]{:S(2)}) collective-permute-start(f32[4,24,128]{2,1,0:T(8,128)S(1)} %pad_maximum_fusion.1), channel_id=1, source_target_pairs={{0,5},{1,4},{2,7},{3,6},{4,1},{5,0},{6,3},{7,2},{8,13},{9,12},{10,... | collective-permute-start | bytes 147464 | tf_op jit(solution)/shard_map/ppermute | solution.py:572
  12.2 1.8 %collective-permute-done.2 = f32[4,24,128]{2,1,0:T(8,128)S(1)} collective-permute-done((f32[4,24,128]{2,1,0:T(8,128)S(1)}, f32[4,24,128]{2,1,0:T(8,128)S(1)}, u32[]{:S(2)}, u32[]{:S(2)}) %collective-permute-start.2) | collective-permute-done | bytes 49184 | tf_op jit(solution)/shard_map/ppermute | solution.py:572
  14.0 0.0 copy-start.5
  14.0 0.5 %collective-permute-start.3 = (f32[8,24,128]{2,1,0:T(8,128)S(1)}, f32[8,24,128]{2,1,0:T(8,128)S(1)}, u32[]{:S(2)}, u32[]{:S(2)}) collective-permute-start(f32[8,24,128]{2,1,0:T(8,128)S(1)} %pad_maximum_fusion.own_ref), channel_id=1, source_target_pairs={{0,1},{1,0},{2,3},{3,2},{4,5},{5,4},{6,7},{7,6},{8,9},{9,8},{10,11... | collective-permute-start | bytes 294920 | tf_op jit(solution)/shard_map/ppermute | solution.py:574
  14.5 0.0 copy-done.2
  14.5 0.1 collective-permute-start.6
  14.6 0.0 copy-done.3
  14.6 0.0 copy-start
  14.6 0.4 %collective-permute-start.5 = (f32[2,2,128]{2,1,0:T(2,128)S(1)}, f32[2,2,128]{2,1,0:T(2,128)S(1)}, u32[]{:S(2)}, u32[]{:S(2)}) collective-permute-start(f32[2,2,128]{2,1,0:T(2,128)S(1)} %bitcast.9), channel_id=1, source_target_pairs={{0,1},{1,0},{2,3},{3,2},{4,5},{5,4},{6,7},{7,6},{8,9},{9,8},{10,11... | collective-permute-start | bytes 6152 | tf_op jit(solution)/shard_map/ppermute | solution.py:554
  15.0 0.0 copy-done.5
  15.1 0.0 copy-start.1
  15.1 1.0 %copy-done.1 = f32[1024,128]{1,0:T(8,128)S(1)} copy-done((f32[1024,128]{1,0:T(8,128)S(1)}, f32[1024,128]{1,0:T(8,128)}, u32[]{:S(2)}) %copy-start.1) | copy-done | bytes 524312
  16.1 0.0 copy-start.4
  16.1 0.8 %table.1 = (bf16[1024,256]{1,0:T(8,128)(2,1)S(1)}, f32[8,128]{1,0:T(8,128)S(1)}) custom-call(f32[1024,128]{1,0:T(8,128)S(1)} %copy-done.1, s32[8]{0:T(128)S(1)} %copy-done.5), custom_call_target="tpu_custom_call" | custom-call | flops 4194304 | bytes 1048576 | tf_op jit(solution)/shard_map/table/pallas_call | solution.py:540
  16.9 0.0 collective-permute-done.5.peer_bias
  16.9 0.0 collective-permute-done.6.peer_out
  17.0 0.0 collective-permute-done.4.peer_in
  17.0 0.0 copy-done
  17.0 0.0 copy-done.4
  17.0 0.5 %shard_map.131 = (bf16[256,640]{1,0:T(8,128)(2,1)S(1)}, bf16[256,128]{1,0:T(8,128)(2,1)S(1)}) custom-call(f32[2,128]{1,0:T(2,128)S(1)} %copy-done.4, f32[2,128,2,128]{3,2,1,0:T(2,128)S(1)} %copy-done, f32[2,128,2,128]{3,2,1,0:T(2,128)S(1)} %collective-permute-done.4.peer_in, f32[2,2,128]{2,1,0:T(2,128)S(1)} %bitcast.10, ...), custom_call_target="tpu_custom_call" | custom-call | flops 4194304 | bytes 1048576 | tf_op jit(solution)/shard_map/pallas_call | solution.py:557
  17.5 0.7 %shard_map.132 = (bf16[256,640]{1,0:T(8,128)(2,1)S(1)}, bf16[256,128]{1,0:T(8,128)(2,1)S(1)}, bf16[256,640]{1,0:T(8,128)(2,1)S(1)}) custom-call(f32[2,128]{1,0:T(2,128)S(1)} %copy-done.4, f32[2,128,2,128]{3,2,1,0:T(2,128)S(1)} %copy-done, f32[2,128,2,128]{3,2,1,0:T(2,128)S(1)} %collective-permute-done.4.peer_in, f32[2,2,128]{2,1,0:T(2,128)S(1)} %bitcast.11, ...), custom_call_target="tpu_custom_call" | custom-call | flops 4194304 | bytes 1048576 | tf_op jit(solution)/shard_map/pallas_call | solution.py:557
  18.2 0.0 collective-permute-done.3.peer_ref
  18.3 4.1 %part.1 = (f32[1,8,128]{2,1,0:T(8,128)}, f32[1,8,128]{2,1,0:T(8,128)}) custom-call(f32[8,24,128]{2,1,0:T(8,128)S(1)} %pad_maximum_fusion.own_ref, f32[8,24,128]{2,1,0:T(8,128)S(1)} %collective-permute-done.3.peer_ref, f32[8,128]{1,0:T(8,128)S(1)} %get-tuple-element.9.live_ref, bf16[256,640]{1,0:T(8,128)(2,1)S(1)} %get-tuple-element.10.in_0, ...), custom_call_target="tpu_custom_call" | custom-call | tf_op jit(solution)/shard_map/part/pallas_call | solution.py:576
  (3 shorter events, 0.0 us)
Async XLA Ops:
  2.0 5.0 %collective-permute-start = (f32[1,24,128]{2,1,0:T(8,128)S(1)}, f32[1,24,128]{2,1,0:T(8,128)S(1)}, u32[]{:S(2)}, u32[]{:S(2)}) collective-permute-start(f32[1,24,128]{2,1,0:T(8,128)S(1)} %bitcast.5), channel_id=1, source_target_pairs={{0,9},{1,8},{2,11},{3,10},{4,13},{5,12},{6,15},{7,14},{8,1},{9,0},... | collective-permute-start | bytes 36872 | tf_op jit(solution)/shard_map/ppermute | solution.py:572
  6.9 3.3 %collective-permute-start.1 = (f32[2,24,128]{2,1,0:T(8,128)S(1)}, f32[2,24,128]{2,1,0:T(8,128)S(1)}, u32[]{:S(2)}, u32[]{:S(2)}) collective-permute-start(f32[2,24,128]{2,1,0:T(8,128)S(1)} %pad_maximum_fusion.2), channel_id=1, source_target_pairs={{0,3},{1,2},{2,1},{3,0},{4,7},{5,6},{6,5},{7,4},{8,11},{9,10},{10,... | collective-permute-start | bytes 73736 | tf_op jit(solution)/shard_map/ppermute | solution.py:572
  8.7 8.2 %collective-permute-start.4 = (f32[2,128,2,128]{3,2,1,0:T(2,128)}, f32[2,128,2,128]{3,2,1,0:T(2,128)S(1)}, u32[]{:S(2)}, u32[]{:S(2)}) collective-permute-start(f32[2,128,2,128]{3,2,1,0:T(2,128)} %own_in.3), channel_id=1, source_target_pairs={{0,1},{1,0},{2,3},{3,2},{4,5},{5,4},{6,7},{7,6},{8,9},{9,8},{10,11... | collective-permute-start | bytes 786440 | tf_op jit(solution)/shard_map/ppermute | solution.py:554
  10.3 4.3 %copy-start.2 = (f32[2,2,32,128]{3,2,1,0:T(8,128)S(1)}, f32[2,2,32,128]{3,2,1,0:T(8,128)}, u32[]{:S(2)}) copy-start(f32[2,2,32,128]{3,2,1,0:T(8,128)} %own_out.3) | copy-start | bytes 196612
  10.3 4.4 %copy-start.3 = (f32[2,128,2]{1,2,0:T(2,128)S(1)}, f32[2,128,2]{1,2,0:T(2,128)}, u32[]{:S(2)}) copy-start(f32[2,128,2]{1,2,0:T(2,128)} %param.21) | copy-start | bytes 6148
  10.3 3.7 %collective-permute-start.2 = (f32[4,24,128]{2,1,0:T(8,128)S(1)}, f32[4,24,128]{2,1,0:T(8,128)S(1)}, u32[]{:S(2)}, u32[]{:S(2)}) collective-permute-start(f32[4,24,128]{2,1,0:T(8,128)S(1)} %pad_maximum_fusion.1), channel_id=1, source_target_pairs={{0,5},{1,4},{2,7},{3,6},{4,1},{5,0},{6,3},{7,2},{8,13},{9,12},{10,... | collective-permute-start | bytes 147464 | tf_op jit(solution)/shard_map/ppermute | solution.py:572
  14.0 1.0 %copy-start.5 = (s32[8]{0:T(128)S(1)}, s32[8]{0:T(128)}, u32[]{:S(2)}) copy-start(s32[8]{0:T(128)} %live_ref.1) | copy-start | bytes 100
  14.0 4.2 %collective-permute-start.3 = (f32[8,24,128]{2,1,0:T(8,128)S(1)}, f32[8,24,128]{2,1,0:T(8,128)S(1)}, u32[]{:S(2)}, u32[]{:S(2)}) collective-permute-start(f32[8,24,128]{2,1,0:T(8,128)S(1)} %pad_maximum_fusion.own_ref), channel_id=1, source_target_pairs={{0,1},{1,0},{2,3},{3,2},{4,5},{5,4},{6,7},{7,6},{8,9},{9,8},{10,11... | collective-permute-start | bytes 294920 | tf_op jit(solution)/shard_map/ppermute | solution.py:574
  14.5 2.4 %collective-permute-start.6 = (f32[2,2,32,128]{3,2,1,0:T(8,128)S(1)}, f32[2,2,32,128]{3,2,1,0:T(8,128)S(1)}, u32[]{:S(2)}, u32[]{:S(2)}) collective-permute-start(f32[2,2,32,128]{3,2,1,0:T(8,128)S(1)} %copy-done.2), channel_id=1, source_target_pairs={{0,1},{1,0},{2,3},{3,2},{4,5},{5,4},{6,7},{7,6},{8,9},{9,8},{10,11... | collective-permute-start | bytes 196616 | tf_op jit(solution)/shard_map/ppermute | solution.py:554
  14.6 2.4 %copy-start = (f32[2,128,2,128]{3,2,1,0:T(2,128)S(1)}, f32[2,128,2,128]{3,2,1,0:T(2,128)}, u32[]{:S(2)}) copy-start(f32[2,128,2,128]{3,2,1,0:T(2,128)} %own_in.3) | copy-start | bytes 786436
  14.6 2.3 %collective-permute-start.5 = (f32[2,2,128]{2,1,0:T(2,128)S(1)}, f32[2,2,128]{2,1,0:T(2,128)S(1)}, u32[]{:S(2)}, u32[]{:S(2)}) collective-permute-start(f32[2,2,128]{2,1,0:T(2,128)S(1)} %bitcast.9), channel_id=1, source_target_pairs={{0,1},{1,0},{2,3},{3,2},{4,5},{5,4},{6,7},{7,6},{8,9},{9,8},{10,11... | collective-permute-start | bytes 6152 | tf_op jit(solution)/shard_map/ppermute | solution.py:554
  15.1 1.0 %copy-start.1 = (f32[1024,128]{1,0:T(8,128)S(1)}, f32[1024,128]{1,0:T(8,128)}, u32[]{:S(2)}) copy-start(f32[1024,128]{1,0:T(8,128)} %table_ref.1) | copy-start | bytes 1572868
  16.1 0.9 %copy-start.4 = (f32[2,128]{1,0:T(2,128)S(1)}, f32[2,128]{1,0:T(2,128)}, u32[]{:S(2)}) copy-start(f32[2,128]{1,0:T(2,128)} %gain_ref.3) | copy-start | bytes 3076
